TPU v7x, 512 devices: a whole 4x8x8 slice. The times are simulated.
512 devices in a mesh: gx: 32 (over x, z), gy: 8 (over y_lo, core), gz: 2 (over y_hi).
Axes of the slice: x: 4, y: 8 (y_hi: 2, y_lo: 4; y = y_hi * 4 + y_lo), z: 8, core: 2. Of those that a mesh axis runs over, the one named last changes fastest.
Arguments:
- positions: float32 [64, 32, 8, 8, 3], P('gx', 'gy', 'gz'), may hold values from 0 to 1
- species: int32 [64, 32, 8, 8], P('gx', 'gy', 'gz'), may hold values from 0 to 3
- neighbors: int32 [64, 32, 8, 8, 16], P('gx', 'gy', 'gz'), may hold values from 0 to 215, as said below
- edge_mask: int32 [64, 32, 8, 8, 16], P('gx', 'gy', 'gz'), may hold values 0 or 1
- species_embed: float32 [4, 128], replicated, may hold values from -6 to 6
- radial_weight: float32 [2, 8, 384], replicated, may hold values from -6 to 6
- mix_weight: float32 [2, 384, 128], replicated, may hold values from -0.3125 to 0.3125
- readout: float32 [128], replicated, may hold values from -0.5 to 0.5
- energy_offset: float32 [4], replicated, may hold values from -6 to 6
Outputs:
- atom_energy: float32 [64, 32, 8, 8], P('gx', 'gy', 'gz')
- forces: float32 [64, 32, 8, 8, 3], P('gx', 'gy', 'gz')
Inputs may be any that keep to these rules, and one draw needn't show every extreme that they name: `neighbors`: each entry lies in 0 to 215 and names slot n mod 8 of the cell at offset (n // 72 - 1, (n // 24) mod 3 - 1, (n // 8) mod 3 - 1), periodic; it never names the receiving atom itself (104 plus its own slot). Repeats may occur.
All inputs are finite; a program needn't handle non-finite values.
Results may differ from a plain program's by a relative error of at most 0.0003.
Values sent between devices are 32-bit elements.
No kernel may reach another device: no remote copies, remote signals or barrier semaphores. Data moves between devices by JAX's collectives and lax.ppermute only.
A program may use at most 128 MiB of HBM per device.

v0:
```python
import math

import jax
import jax.numpy as jnp
from jax import lax
from jax.sharding import PartitionSpec as P

cutoff_radius = 2.0
highest = lax.Precision.HIGHEST


def padded(x, sides, width, wrap):
    for axis, dim in sides:
        count, length = lax.axis_size(axis), x.shape[dim]
        up = [(i, (i + 1) % count) for i in range(count if wrap else count - 1)]
        down = [(j, i) for i, j in up]
        last = lax.slice_in_dim(x, length - width, length, axis=dim)
        initial = lax.slice_in_dim(x, 0, width, axis=dim)
        before = lax.ppermute(last, axis, up)
        after = lax.ppermute(initial, axis, down)
        x = jnp.concatenate([before, x, after], axis=dim)
    return x


def stencil_parts(neighbor_ids, slot_count):
    stencil = neighbor_ids // slot_count
    return (stencil // 9 - 1, stencil // 3 % 3 - 1, stencil % 3 - 1, neighbor_ids % slot_count)


def sender_rows(neighbor_ids, grid_y, grid_z, margin):
    arr_shape = neighbor_ids.shape
    slot_count = arr_shape[3]
    step_x, step_y, step_z, slot_id = stencil_parts(neighbor_ids, slot_count)
    cell_x = lax.broadcasted_iota(jnp.int32, arr_shape, 0) + margin + step_x
    cell_y = lax.broadcasted_iota(jnp.int32, arr_shape, 1) + margin + step_y
    cell_z = lax.broadcasted_iota(jnp.int32, arr_shape, 2) + margin + step_z
    return ((cell_x * grid_y + cell_y) * grid_z + cell_z) * slot_count + slot_id


def displacement(pos_padded, pos_own, neighbor_ids, sender_idx):
    step_x, step_y, step_z, slot_id = stencil_parts(neighbor_ids, neighbor_ids.shape[3])
    offsets = jnp.stack([step_x, step_y, step_z], -1).astype(jnp.float32)
    remote = pos_padded.reshape(-1, 3)[sender_idx]
    return offsets + remote - pos_own[..., None, :]


def edge_basis(displace, basis_count):
    radius_sq = jnp.sum(displace * displace, -1)
    radius = jnp.sqrt(radius_sq)
    envelope = jnp.where(radius < cutoff_radius, (1.0 - radius_sq / cutoff_radius**2) ** 2, 0.0)
    centres = jnp.arange(basis_count, dtype=jnp.float32) * (cutoff_radius / (basis_count - 1))
    sharpness = ((basis_count - 1) / cutoff_radius) ** 2
    radial_basis = jnp.exp(-sharpness * (radius[..., None] - centres) ** 2) * envelope[..., None]
    scaled = displace / cutoff_radius
    along_x = scaled[..., 0]
    along_y = scaled[..., 1]
    along_z = scaled[..., 2]
    first_order = math.sqrt(3.0) * scaled
    root_15 = math.sqrt(15.0)
    second_order = jnp.stack(
        [
            root_15 * along_x * along_y,
            root_15 * along_y * along_z,
            0.5 * math.sqrt(5.0) * (3.0 * along_z * along_z - jnp.sum(scaled * scaled, -1)),
            root_15 * along_x * along_z,
            0.5 * root_15 * (along_x * along_x - along_y * along_y),
        ],
        -1,
    )
    return (radial_basis, first_order, second_order)


def interact(senders, radial_basis, first_order, second_order, edge_mask, radial_w, mix_w):
    channels = senders.shape[-1]
    radial = jnp.einsum("...k,kc->...c", radial_basis, radial_w, precision=highest)
    gate_mask = edge_mask.astype(jnp.float32)[..., None]
    term_zero = gate_mask * radial[..., :channels] * senders
    term_one = gate_mask * radial[..., channels : 2 * channels] * senders
    term_two = gate_mask * radial[..., 2 * channels :] * senders
    norm_scale = senders.shape[-2] ** (-0.5)
    scalar_part = norm_scale * jnp.sum(term_zero, -2)
    vector_part = norm_scale * jnp.einsum(
        "...em,...ec->...mc", first_order, term_one, precision=highest
    )
    tensor_part = norm_scale * jnp.einsum(
        "...em,...ec->...mc", second_order, term_two, precision=highest
    )
    invariants = jnp.concatenate(
        [
            scalar_part,
            jnp.sum(vector_part * vector_part, -2),
            jnp.sum(tensor_part * tensor_part, -2),
        ],
        -1,
    )
    return jax.nn.silu(jnp.einsum("...j,jc->...c", invariants, mix_w, precision=highest))


def fold_dim(extended, axis_dim, send_fn):
    size_dim = extended.shape[axis_dim]
    low_slab = lax.slice_in_dim(extended, 0, 1, axis=axis_dim)
    high_slab = lax.slice_in_dim(extended, size_dim - 1, size_dim, axis=axis_dim)
    arrived = send_fn(jnp.concatenate([low_slab, high_slab], axis_dim))
    from_left = lax.slice_in_dim(arrived, 0, 1, axis=axis_dim)
    from_right = lax.slice_in_dim(arrived, 3, 4, axis=axis_dim)
    inner_part = lax.slice_in_dim(extended, 1, size_dim - 1, axis=axis_dim)
    inner_size = size_dim - 2
    head_part = lax.slice_in_dim(inner_part, 0, 1, axis=axis_dim) + from_left
    middle = lax.slice_in_dim(inner_part, 1, inner_size - 1, axis=axis_dim)
    tail_part = lax.slice_in_dim(inner_part, inner_size - 1, inner_size, axis=axis_dim) + from_right
    return jnp.concatenate([head_part, middle, tail_part], axis_dim)


def fold_features(extended):
    extended = fold_dim(extended, 0, lambda part_slab: padded(part_slab, (("gx", 0),), 1, True))
    extended = fold_dim(extended, 1, lambda part_slab: padded(part_slab, (("gy", 1),), 1, True))
    return fold_dim(extended, 2, lambda part_slab: padded(part_slab, (("gz", 2),), 1, True))


def fold_positions(extended):
    extended = fold_dim(extended, 0, lambda part_slab: padded(part_slab, (("gx", 0),), 1, True))
    extended = fold_dim(extended, 1, lambda part_slab: padded(part_slab, (("gy", 1),), 1, True))
    return fold_dim(extended, 2, lambda part_slab: padded(part_slab, (("gz", 2),), 1, True))


def shards(
    positions,
    species,
    neighbors,
    edge_mask,
    species_embed,
    radial_weight,
    mix_weight,
    readout,
    energy_offset,
):
    cells_x = neighbors.shape[0]
    cells_y = neighbors.shape[1]
    cells_z = neighbors.shape[2]
    slot_count = neighbors.shape[3]
    channels = species_embed.shape[1]
    basis_count = radial_weight.shape[1]
    start_feat = species_embed[species]
    near_all = padded(
        jnp.concatenate([positions, start_feat], -1), (("gx", 0), ("gy", 1), ("gz", 2)), 1, True
    )
    pos_near = near_all[..., :3]
    feat_near = near_all[..., 3:]
    sender_idx = sender_rows(neighbors, cells_y + 2, cells_z + 2, 1)
    displace = displacement(pos_near, positions, neighbors, sender_idx)
    geometry, geo_pull = jax.vjp(lambda offsets_in: edge_basis(offsets_in, basis_count), displace)

    def layer_apply(feat_ext, geom_in, layer_idx):
        senders = feat_ext.reshape(-1, channels)[sender_idx]
        return interact(
            senders,
            geom_in[0],
            geom_in[1],
            geom_in[2],
            edge_mask,
            radial_weight[layer_idx],
            mix_weight[layer_idx],
        )

    update_one, pull_one = jax.vjp(lambda geom_in: layer_apply(feat_near, geom_in, 0), geometry)
    hidden_one = start_feat + update_one
    hidden_near = padded(hidden_one, (("gx", 0), ("gy", 1), ("gz", 2)), 1, True)
    update_two, pull_two = jax.vjp(
        lambda feat_ext, geom_in: layer_apply(feat_ext, geom_in, 1), hidden_near, geometry
    )
    hidden_two = hidden_one + update_two
    energy = energy_offset[species] + jnp.einsum(
        "...c,c->...", hidden_two, readout, precision=highest
    )
    cot_two = jnp.broadcast_to(readout, hidden_two.shape)
    cot_near, geo_two = pull_two(cot_two)
    cot_one = cot_two + fold_features(cot_near)
    (geo_one,) = pull_one(cot_one)
    geo_sum = jax.tree.map(lambda term_a, term_b: term_a + term_b, geo_one, geo_two)
    (edge_grad,) = geo_pull(geo_sum)
    received = jnp.sum(edge_grad, -2)
    sums_near = jax.ops.segment_sum(
        edge_grad.reshape(-1, 3),
        sender_idx.reshape(-1),
        num_segments=(cells_x + 2) * (cells_y + 2) * (cells_z + 2) * slot_count,
    )
    sent_back = fold_positions(
        sums_near.reshape(cells_x + 2, cells_y + 2, cells_z + 2, slot_count, 3)
    )
    return (energy, received - sent_back)


def solution(mesh):
    in_specs = (
        P("gx", "gy", "gz", None, None),
        P("gx", "gy", "gz", None),
        P("gx", "gy", "gz", None, None),
        P("gx", "gy", "gz", None, None),
        P(),
        P(),
        P(),
        P(),
        P(),
    )
    out_specs = (P("gx", "gy", "gz", None), P("gx", "gy", "gz", None, None))
    return jax.shard_map(shards, mesh=mesh, in_specs=in_specs, out_specs=out_specs, check_vma=False)
```

profile of v0, /device:TPU:1, one launch (start us, length us, event | category | flops | bytes accessed | tf_op | source)
XLA Modules:
  0.0 402.6 jit_solution(17478479482609436192)
XLA Ops:
  8.3 10.8 %collective-permute-start.1 = (f32[1,4,4,8,131]{4,3,2,1,0:T(8,128)S(1)}, f32[1,4,4,8,131]{4,3,2,1,0:T(8,128)S(1)}, u32[]{:S(2)}, u32[]{:S(2)}) collective-permute-start(f32[1,4,4,8,131]{4,3,2,1,0:T(8,128)S(1)} %get-tuple-element.64), channel_id=1, source_target_pairs={{16,0},{32,16},{48,32},{64,48},{80,64},{96,80},{112,96},{128,112},... | collective-permute-start | bytes 201224 | tf_op jit(solution)/shard_map/ppermute | solution.py:20
  32.7 6.9 %collective-permute-start.4 = (f32[4,6,1,8,131]{4,3,2,1,0:T(8,128)S(1)}, f32[4,6,1,8,131]{4,3,2,1,0:T(8,128)S(1)}, u32[]{:S(2)}, u32[]{:S(2)}) collective-permute-start(f32[4,6,1,8,131]{4,3,2,1,0:T(8,128)S(1)} %get-tuple-element.34), channel_id=1, source_target_pairs={{0,1},{1,0},{2,3},{3,2},{4,5},{5,4},{6,7},{7,6},{8,9},{9,8},{10,11... | collective-permute-start | bytes 301832 | tf_op jit(solution)/shard_map/ppermute | solution.py:19
  41.9 6.0 %collective-permute-done.4 = f32[4,6,1,8,131]{4,3,2,1,0:T(8,128)S(1)} collective-permute-done((f32[4,6,1,8,131]{4,3,2,1,0:T(8,128)S(1)}, f32[4,6,1,8,131]{4,3,2,1,0:T(8,128)S(1)}, u32[]{:S(2)}, u32[]{:S(2)}) %collective-permute-start.4) | collective-permute-done | bytes 100640 | tf_op jit(solution)/shard_map/ppermute | solution.py:19
  47.9 8.7 %collective-permute-done.5 = f32[4,6,1,8,131]{4,3,2,1,0:T(8,128)S(1)} collective-permute-done((f32[4,6,1,8,131]{4,3,2,1,0:T(8,128)S(1)}, f32[4,6,1,8,131]{4,3,2,1,0:T(8,128)S(1)}, u32[]{:S(2)}, u32[]{:S(2)}) %collective-permute-start.5) | collective-permute-done | bytes 100640 | tf_op jit(solution)/shard_map/ppermute | solution.py:20
  57.1 10.8 %gather_fusion.3 = f32[4096,128]{1,0:T(8,128)S(1)} fusion(f32[1152,128]{1,0:T(8,128)S(1)} %bitcast.89, s32[4096]{0:T(1024)S(1)} %broadcast_clamp_fusion), kind=kCustom, calls=%fused_computation.3 | custom fusion | bytes 4210688 | tf_op jit(solution)/shard_map/jvp()/gather | solution.py:154
  67.9 14.1 %gather_fusion.2 = f32[4096,3]{1,0:T(8,128)} fusion(f32[1152,3]{1,0:T(8,128)S(1)} %bitcast.88, s32[4096]{0:T(1024)S(1)} %broadcast_clamp_fusion), kind=kCustom, calls=%fused_computation.2 | custom fusion | bytes 114688 | tf_op jit(solution)/shard_map/gather | solution.py:43
  88.1 5.8 %fusion.35 = f32[2,4,4,8,16,384]{5,4,3,2,1,0:T(8,128)S(1)} fusion(f32[2,4,4,8,16]{4,3,2,1,0:T(8,128)S(1)} %get-tuple-element.72, f32[8]{0:T(128)S(1)} %iota_multiply_fusion, f32[2,4,4,8,16]{4,3,2,1,0:T(8,128)S(1)} %get-tuple-element.71, f32[2,8,384]{2,1,0:T(8,128)S(1)} %copy-done.43), kind=kOutput, calls=%fused_computation.56 | convolution fusion | flops 151126016 | bytes 6566400 | tf_op jit(solution)/shard_map/jvp(...k,kc->...c)/dot_general | solution.py:75
  105.1 7.5 %collective-permute-start.7 = (f32[1,4,4,8,128]{4,3,2,1,0:T(8,128)S(1)}, f32[1,4,4,8,128]{4,3,2,1,0:T(8,128)S(1)}, u32[]{:S(2)}, u32[]{:S(2)}) collective-permute-start(f32[1,4,4,8,128]{4,3,2,1,0:T(8,128)S(1)} %get-tuple-element.70), channel_id=1, source_target_pairs={{16,0},{32,16},{48,32},{64,48},{80,64},{96,80},{112,96},{128,112},... | collective-permute-start | bytes 196616 | tf_op jit(solution)/shard_map/ppermute | solution.py:20
  124.0 7.7 %collective-permute-start.10 = (f32[4,6,1,8,128]{4,3,2,1,0:T(8,128)S(1)}, f32[4,6,1,8,128]{4,3,2,1,0:T(8,128)S(1)}, u32[]{:S(2)}, u32[]{:S(2)}) collective-permute-start(f32[4,6,1,8,128]{4,3,2,1,0:T(8,128)S(1)} %get-tuple-element.53), channel_id=1, source_target_pairs={{0,1},{1,0},{2,3},{3,2},{4,5},{5,4},{6,7},{7,6},{8,9},{9,8},{10,11... | collective-permute-start | bytes 294920 | tf_op jit(solution)/shard_map/ppermute | solution.py:19
  133.7 7.4 %fusion.33 = f32[2,4,4,8,16,384]{5,4,3,2,1,0:T(8,128)} fusion(f32[2,4,4,8,16]{4,3,2,1,0:T(8,128)S(1)} %copy-done.28, f32[8]{0:T(128)S(1)} %iota_multiply_fusion, f32[2,4,4,8,16]{4,3,2,1,0:T(8,128)S(1)} %copy-done.25, f32[2,8,384]{2,1,0:T(8,128)S(1)} %copy-done.43), kind=kOutput, calls=%fused_computation.55 | convolution fusion | flops 151126016 | bytes 6566400 | tf_op jit(solution)/shard_map/jvp(...k,kc->...c)/dot_general | solution.py:75
  143.3 14.1 %gather_fusion.4 = f32[4096,128]{1,0:T(8,128)} fusion(f32[1152,128]{1,0:T(8,128)S(1)} %bitcast.87, s32[4096]{0:T(1024)S(1)} %broadcast_clamp_fusion), kind=kCustom, calls=%fused_computation.4 | custom fusion | bytes 4210688 | tf_op jit(solution)/shard_map/jvp()/gather | solution.py:154
  173.2 7.3 %multiply_add_fusion = (f32[2,4,4,8,16,128]{5,4,3,2,1,0:T(8,128)}, f32[2,4,4,8,16,128]{5,4,3,2,1,0:T(8,128)}, f32[2,4,4,8,16,128]{5,4,3,2,1,0:T(8,128)}, f32[2,4,4,8,16,128]{5,4,3,2,1,0:T(8,128)}) fusion(f32[2,4,4,8,16,128]{5,4,3,2,1,0:T(8,128)S(1)} %fusion.19, f32[2,4,4,8,16,384]{5,4,3,2,1,0:T(8,128)S(1)} %copy-done.4, ...), kind=kOutput, calls=%fused_computation.35 | convolution fusion | flops 26509312 | bytes 21692416 | tf_op jit(solution)/shard_map/transpose(jvp(...em,...ec->...mc))/dot_general | solution.py:82
  180.5 23.7 %scatter_custom_fusion = f32[1152,128]{1,0:T(8,128)} fusion(s32[4096]{0:T(1024)} %copy-done.42, f32[4096,128]{1,0:T(8,128)} %bitcast.109, f32[]{:T(128)} %constant.102.clone.1), kind=kCustom, calls=%fused_computation.134 | custom fusion | flops 524288 | bytes 590336 | tf_op jit(solution)/shard_map/transpose(jvp())/scatter-add | solution.py:154
  205.4 6.5 %collective-permute-start.13 = (f32[1,6,6,8,128]{4,3,2,1,0:T(8,128)S(1)}, f32[1,6,6,8,128]{4,3,2,1,0:T(8,128)S(1)}, u32[]{:S(2)}, u32[]{:S(2)}) collective-permute-start(f32[1,6,6,8,128]{4,3,2,1,0:T(8,128)S(1)} %bitcast.117), channel_id=1, source_target_pairs={{16,0},{32,16},{48,32},{64,48},{80,64},{96,80},{112,96},{128,112},... | collective-permute-start | bytes 442376 | tf_op jit(solution)/shard_map/ppermute | solution.py:20
  213.9 6.3 %fusion.41 = f32[2,4,4,8,16,5]{4,5,3,2,1,0:T(8,128)S(1)} fusion(f32[2,4,4,8,5,128]{5,4,3,2,1,0:T(8,128)} %copy-done.11, f32[2,4,4,8,16,128]{5,4,3,2,1,0:T(8,128)} %bitcast.96, f32[2,4,4,8,16,384]{5,4,3,2,1,0:T(8,128)} %fusion.33, f32[2,4,4,8,16]{4,3,2,1,0:T(8,128)S(1)} %convert_element_type.7, f32[2,4,4,8,128]{4,3,2,1,0:T(8,128)S(1)} %get-tuple-element.50), kind=kOutput, calls=%fused_computation.65 | convolution fusion | flops 32997376 | bytes 5472256 | tf_op jit(solution)/shard_map/transpose(jvp(...em,...ec->...mc))/dot_general | solution.py:85
  221.2 5.4 %collective-permute-start.14 = (f32[2,1,6,8,128]{4,3,2,1,0:T(8,128)S(1)}, f32[2,1,6,8,128]{4,3,2,1,0:T(8,128)S(1)}, u32[]{:S(2)}, u32[]{:S(2)}) collective-permute-start(f32[2,1,6,8,128]{4,3,2,1,0:T(8,128)S(1)} %pad_maximum_fusion.26), channel_id=1, source_target_pairs={{0,2},{2,4},{4,6},{6,8},{8,10},{10,12},{12,14},{14,0},{1,3},{3,5},... | collective-permute-start | bytes 147464 | tf_op jit(solution)/shard_map/ppermute | solution.py:19
  226.6 5.2 %fusion.45 = f32[2,4,4,8,16,3]{4,5,3,2,1,0:T(4,128)S(1)} fusion(f32[2,4,4,8,16,128]{5,4,3,2,1,0:T(8,128)S(1)} %bitcast.100, f32[2,4,4,8,16,384]{5,4,3,2,1,0:T(8,128)} %fusion.33, f32[2,4,4,8,16]{4,3,2,1,0:T(8,128)S(1)} %convert_element_type.7, f32[2,4,4,8,3,128]{5,4,3,2,1,0:T(4,128)S(1)} %copy-done.13, f32[2,4,4,8,128]{4,3,2,1,0:T(8,128)S(1)} %get-tuple-element.52), kind=kOutput, calls=%fused_computation.68 | convolution fusion | flops 20217856 | bytes 4784128 | tf_op jit(solution)/shard_map/transpose(jvp(...em,...ec->...mc))/dot_general | solution.py:82
  237.3 6.6 %collective-permute-start.16 = (f32[2,4,1,8,128]{4,3,2,1,0:T(8,128)S(1)}, f32[2,4,1,8,128]{4,3,2,1,0:T(8,128)S(1)}, u32[]{:S(2)}, u32[]{:S(2)}) collective-permute-start(f32[2,4,1,8,128]{4,3,2,1,0:T(8,128)S(1)} %pad_maximum_fusion.30), channel_id=1, source_target_pairs={{0,1},{1,0},{2,3},{3,2},{4,5},{5,4},{6,7},{7,6},{8,9},{9,8},{10,11... | collective-permute-start | bytes 98312 | tf_op jit(solution)/shard_map/ppermute | solution.py:19
  243.9 29.4 %fusion = f32[2,4,4,8,16,8]{4,5,3,2,1,0:T(8,128)S(1)} fusion(f32[2,4,4,8,16,128]{5,4,3,2,1,0:T(8,128)S(1)} %copy-done.21, f32[2,4,4,8,16,128]{5,4,3,2,1,0:T(8,128)S(1)} %copy-done.20, f32[2,4,4,8,16,128]{5,4,3,2,1,0:T(8,128)S(1)} %copy-done.19, f32[2,8,384]{2,1,0:T(8,128)S(1)} %copy-done.44), kind=kOutput, calls=%fused_computation.7 | convolution fusion | flops 154140672 | bytes 6434816 | tf_op jit(solution)/shard_map/transpose(jvp(...k,kc->...c))/dot_general | solution.py:75
  276.9 5.2 %collective-permute-done.17 = f32[2,4,1,8,128]{4,3,2,1,0:T(8,128)S(1)} collective-permute-done((f32[2,4,1,8,128]{4,3,2,1,0:T(8,128)S(1)}, f32[2,4,1,8,128]{4,3,2,1,0:T(8,128)S(1)}, u32[]{:S(2)}, u32[]{:S(2)}) %collective-permute-start.17) | collective-permute-done | bytes 32800 | tf_op jit(solution)/shard_map/ppermute | solution.py:20
  300.6 29.4 %fusion.37 = (f32[2,4,4,8,16]{4,3,2,1,0:T(8,128)S(1)}, f32[2,4,4,8,16]{4,3,2,1,0:T(8,128)S(1)}) fusion(f32[8]{0:T(128)S(1)} %iota_multiply_fusion, f32[2,4,4,8,16]{4,3,2,1,0:T(8,128)S(1)} %copy-done.26, f32[2,4,4,8,16]{4,3,2,1,0:T(8,128)S(1)} %copy-done.29, f32[2,4,4,8,16,8]{4,5,3,2,1,0:T(8,128)S(1)} %fusion, f32[2,8,384]{2,1,0:T(8,128)S(1)} %copy-done.44, ...), kind=kOutput, calls=%fused_computation.57 | convolution fusion | flops 154525696 | bytes 7647744 | tf_op jit(solution)/shard_map/transpose(jvp(...k,kc->...c))/dot_general | solution.py:75
  332.0 22.6 %scatter_custom_fusion.1 = f32[1152,3]{1,0:T(8,128)S(1)} fusion(s32[4096]{0:T(1024)} %reshape.110, f32[4096,3]{1,0:T(8,128)S(1)} %bitcast.110, f32[]{:T(128)} %constant.102.clone.1), kind=kCustom, calls=%fused_computation.132 | custom fusion | flops 12288 | bytes 14336 | tf_op jit(solution)/shard_map/scatter-add | solution.py:182
  361.7 7.1 %collective-permute-done.18 = f32[1,6,6,8,3]{4,3,2,1,0:T(8,128)S(1)} collective-permute-done((f32[1,6,6,8,3]{4,3,2,1,0:T(8,128)S(1)}, f32[1,6,6,8,3]{4,3,2,1,0:T(8,128)S(1)}, u32[]{:S(2)}, u32[]{:S(2)}) %collective-permute-start.18) | collective-permute-done | bytes 3488 | tf_op jit(solution)/shard_map/ppermute | solution.py:19
  377.0 6.5 %collective-permute-start.21 = (f32[2,1,6,8,3]{4,3,2,1,0:T(8,128)S(1)}, f32[2,1,6,8,3]{4,3,2,1,0:T(8,128)S(1)}, u32[]{:S(2)}, u32[]{:S(2)}) collective-permute-start(f32[2,1,6,8,3]{4,3,2,1,0:T(8,128)S(1)} %get-tuple-element.57), channel_id=1, source_target_pairs={{2,0},{4,2},{6,4},{8,6},{10,8},{12,10},{14,12},{0,14},{3,1},{5,3},... | collective-permute-start | bytes 3464 | tf_op jit(solution)/shard_map/ppermute | solution.py:20
  (224 shorter events, 139.8 us)
Async XLA Ops:
  3.5 17.9 %collective-permute-start = (f32[1,4,4,8,131]{4,3,2,1,0:T(8,128)S(1)}, f32[1,4,4,8,131]{4,3,2,1,0:T(8,128)S(1)}, u32[]{:S(2)}, u32[]{:S(2)}) collective-permute-start(f32[1,4,4,8,131]{4,3,2,1,0:T(8,128)S(1)} %get-tuple-element.63), channel_id=1, source_target_pairs={{0,16},{16,32},{32,48},{48,64},{64,80},{80,96},{96,112},{112,128},... | collective-permute-start | bytes 201224 | tf_op jit(solution)/shard_map/ppermute | solution.py:19
  8.3 13.1 %collective-permute-start.1 = (f32[1,4,4,8,131]{4,3,2,1,0:T(8,128)S(1)}, f32[1,4,4,8,131]{4,3,2,1,0:T(8,128)S(1)}, u32[]{:S(2)}, u32[]{:S(2)}) collective-permute-start(f32[1,4,4,8,131]{4,3,2,1,0:T(8,128)S(1)} %get-tuple-element.64), channel_id=1, source_target_pairs={{16,0},{32,16},{48,32},{64,48},{80,64},{96,80},{112,96},{128,112},... | collective-permute-start | bytes 201224 | tf_op jit(solution)/shard_map/ppermute | solution.py:20
  21.5 6.9 %collective-permute-start.2 = (f32[4,1,4,8,131]{4,3,2,1,0:T(8,128)S(1)}, f32[4,1,4,8,131]{4,3,2,1,0:T(8,128)S(1)}, u32[]{:S(2)}, u32[]{:S(2)}) collective-permute-start(f32[4,1,4,8,131]{4,3,2,1,0:T(8,128)S(1)} %get-tuple-element.45), channel_id=1, source_target_pairs={{0,2},{2,4},{4,6},{6,8},{8,10},{10,12},{12,14},{14,0},{1,3},{3,5},... | collective-permute-start | bytes 201224 | tf_op jit(solution)/shard_map/ppermute | solution.py:19
  26.3 6.3 %collective-permute-start.3 = (f32[4,1,4,8,131]{4,3,2,1,0:T(8,128)S(1)}, f32[4,1,4,8,131]{4,3,2,1,0:T(8,128)S(1)}, u32[]{:S(2)}, u32[]{:S(2)}) collective-permute-start(f32[4,1,4,8,131]{4,3,2,1,0:T(8,128)S(1)} %get-tuple-element.46), channel_id=1, source_target_pairs={{2,0},{4,2},{6,4},{8,6},{10,8},{12,10},{14,12},{0,14},{3,1},{5,3},... | collective-permute-start | bytes 201224 | tf_op jit(solution)/shard_map/ppermute | solution.py:20
  32.7 15.2 %collective-permute-start.4 = (f32[4,6,1,8,131]{4,3,2,1,0:T(8,128)S(1)}, f32[4,6,1,8,131]{4,3,2,1,0:T(8,128)S(1)}, u32[]{:S(2)}, u32[]{:S(2)}) collective-permute-start(f32[4,6,1,8,131]{4,3,2,1,0:T(8,128)S(1)} %get-tuple-element.34), channel_id=1, source_target_pairs={{0,1},{1,0},{2,3},{3,2},{4,5},{5,4},{6,7},{7,6},{8,9},{9,8},{10,11... | collective-permute-start | bytes 301832 | tf_op jit(solution)/shard_map/ppermute | solution.py:19
  39.7 17.0 %collective-permute-start.5 = (f32[4,6,1,8,131]{4,3,2,1,0:T(8,128)S(1)}, f32[4,6,1,8,131]{4,3,2,1,0:T(8,128)S(1)}, u32[]{:S(2)}, u32[]{:S(2)}) collective-permute-start(f32[4,6,1,8,131]{4,3,2,1,0:T(8,128)S(1)} %get-tuple-element.35), channel_id=1, source_target_pairs={{1,0},{0,1},{3,2},{2,3},{5,4},{4,5},{7,6},{6,7},{9,8},{8,9},{11,10... | collective-permute-start | bytes 301832 | tf_op jit(solution)/shard_map/ppermute | solution.py:20
  103.2 9.4 %collective-permute-start.6 = (f32[1,4,4,8,128]{4,3,2,1,0:T(8,128)S(1)}, f32[1,4,4,8,128]{4,3,2,1,0:T(8,128)S(1)}, u32[]{:S(2)}, u32[]{:S(2)}) collective-permute-start(f32[1,4,4,8,128]{4,3,2,1,0:T(8,128)S(1)} %get-tuple-element.69), channel_id=1, source_target_pairs={{0,16},{16,32},{32,48},{48,64},{64,80},{80,96},{96,112},{112,128},... | collective-permute-start | bytes 196616 | tf_op jit(solution)/shard_map/ppermute | solution.py:19
  105.1 8.8 %collective-permute-start.7 = (f32[1,4,4,8,128]{4,3,2,1,0:T(8,128)S(1)}, f32[1,4,4,8,128]{4,3,2,1,0:T(8,128)S(1)}, u32[]{:S(2)}, u32[]{:S(2)}) collective-permute-start(f32[1,4,4,8,128]{4,3,2,1,0:T(8,128)S(1)} %get-tuple-element.70), channel_id=1, source_target_pairs={{16,0},{32,16},{48,32},{64,48},{80,64},{96,80},{112,96},{128,112},... | collective-permute-start | bytes 196616 | tf_op jit(solution)/shard_map/ppermute | solution.py:20
  113.9 8.1 %collective-permute-start.8 = (f32[4,1,4,8,128]{4,3,2,1,0:T(8,128)S(1)}, f32[4,1,4,8,128]{4,3,2,1,0:T(8,128)S(1)}, u32[]{:S(2)}, u32[]{:S(2)}) collective-permute-start(f32[4,1,4,8,128]{4,3,2,1,0:T(8,128)S(1)} %get-tuple-element.61), channel_id=1, source_target_pairs={{0,2},{2,4},{4,6},{6,8},{8,10},{10,12},{12,14},{14,0},{1,3},{3,5},... | collective-permute-start | bytes 196616 | tf_op jit(solution)/shard_map/ppermute | solution.py:19
  118.4 5.6 %collective-permute-start.9 = (f32[4,1,4,8,128]{4,3,2,1,0:T(8,128)S(1)}, f32[4,1,4,8,128]{4,3,2,1,0:T(8,128)S(1)}, u32[]{:S(2)}, u32[]{:S(2)}) collective-permute-start(f32[4,1,4,8,128]{4,3,2,1,0:T(8,128)S(1)} %get-tuple-element.62), channel_id=1, source_target_pairs={{2,0},{4,2},{6,4},{8,6},{10,8},{12,10},{14,12},{0,14},{3,1},{5,3},... | collective-permute-start | bytes 196616 | tf_op jit(solution)/shard_map/ppermute | solution.py:20
  124.0 17.0 %collective-permute-start.10 = (f32[4,6,1,8,128]{4,3,2,1,0:T(8,128)S(1)}, f32[4,6,1,8,128]{4,3,2,1,0:T(8,128)S(1)}, u32[]{:S(2)}, u32[]{:S(2)}) collective-permute-start(f32[4,6,1,8,128]{4,3,2,1,0:T(8,128)S(1)} %get-tuple-element.53), channel_id=1, source_target_pairs={{0,1},{1,0},{2,3},{3,2},{4,5},{5,4},{6,7},{7,6},{8,9},{9,8},{10,11... | collective-permute-start | bytes 294920 | tf_op jit(solution)/shard_map/ppermute | solution.py:19
  131.8 10.6 %collective-permute-start.11 = (f32[4,6,1,8,128]{4,3,2,1,0:T(8,128)S(1)}, f32[4,6,1,8,128]{4,3,2,1,0:T(8,128)S(1)}, u32[]{:S(2)}, u32[]{:S(2)}) collective-permute-start(f32[4,6,1,8,128]{4,3,2,1,0:T(8,128)S(1)} %get-tuple-element.54), channel_id=1, source_target_pairs={{1,0},{0,1},{3,2},{2,3},{5,4},{4,5},{7,6},{6,7},{9,8},{8,9},{11,10... | collective-permute-start | bytes 294920 | tf_op jit(solution)/shard_map/ppermute | solution.py:20
  205.4 14.8 %collective-permute-start.13 = (f32[1,6,6,8,128]{4,3,2,1,0:T(8,128)S(1)}, f32[1,6,6,8,128]{4,3,2,1,0:T(8,128)S(1)}, u32[]{:S(2)}, u32[]{:S(2)}) collective-permute-start(f32[1,6,6,8,128]{4,3,2,1,0:T(8,128)S(1)} %bitcast.117), channel_id=1, source_target_pairs={{16,0},{32,16},{48,32},{64,48},{80,64},{96,80},{112,96},{128,112},... | collective-permute-start | bytes 442376 | tf_op jit(solution)/shard_map/ppermute | solution.py:20
  211.8 9.3 %collective-permute-start.12 = (f32[1,6,6,8,128]{4,3,2,1,0:T(8,128)S(1)}, f32[1,6,6,8,128]{4,3,2,1,0:T(8,128)S(1)}, u32[]{:S(2)}, u32[]{:S(2)}) collective-permute-start(f32[1,6,6,8,128]{4,3,2,1,0:T(8,128)S(1)} %bitcast.115), channel_id=1, source_target_pairs={{0,16},{16,32},{32,48},{48,64},{64,80},{80,96},{96,112},{112,128},... | collective-permute-start | bytes 442376 | tf_op jit(solution)/shard_map/ppermute | solution.py:19
  221.2 10.6 %collective-permute-start.14 = (f32[2,1,6,8,128]{4,3,2,1,0:T(8,128)S(1)}, f32[2,1,6,8,128]{4,3,2,1,0:T(8,128)S(1)}, u32[]{:S(2)}, u32[]{:S(2)}) collective-permute-start(f32[2,1,6,8,128]{4,3,2,1,0:T(8,128)S(1)} %pad_maximum_fusion.26), channel_id=1, source_target_pairs={{0,2},{2,4},{4,6},{6,8},{8,10},{10,12},{12,14},{14,0},{1,3},{3,5},... | collective-permute-start | bytes 147464 | tf_op jit(solution)/shard_map/ppermute | solution.py:19
  231.9 5.4 %collective-permute-start.15 = (f32[2,1,6,8,128]{4,3,2,1,0:T(8,128)S(1)}, f32[2,1,6,8,128]{4,3,2,1,0:T(8,128)S(1)}, u32[]{:S(2)}, u32[]{:S(2)}) collective-permute-start(f32[2,1,6,8,128]{4,3,2,1,0:T(8,128)S(1)} %get-tuple-element.59), channel_id=1, source_target_pairs={{2,0},{4,2},{6,4},{8,6},{10,8},{12,10},{14,12},{0,14},{3,1},{5,3},... | collective-permute-start | bytes 147464 | tf_op jit(solution)/shard_map/ppermute | solution.py:20
  237.3 36.1 %collective-permute-start.16 = (f32[2,4,1,8,128]{4,3,2,1,0:T(8,128)S(1)}, f32[2,4,1,8,128]{4,3,2,1,0:T(8,128)S(1)}, u32[]{:S(2)}, u32[]{:S(2)}) collective-permute-start(f32[2,4,1,8,128]{4,3,2,1,0:T(8,128)S(1)} %pad_maximum_fusion.30), channel_id=1, source_target_pairs={{0,1},{1,0},{2,3},{3,2},{4,5},{5,4},{6,7},{7,6},{8,9},{9,8},{10,11... | collective-permute-start | bytes 98312 | tf_op jit(solution)/shard_map/ppermute | solution.py:19
  273.4 8.7 %collective-permute-start.17 = (f32[2,4,1,8,128]{4,3,2,1,0:T(8,128)S(1)}, f32[2,4,1,8,128]{4,3,2,1,0:T(8,128)S(1)}, u32[]{:S(2)}, u32[]{:S(2)}) collective-permute-start(f32[2,4,1,8,128]{4,3,2,1,0:T(8,128)S(1)} %get-tuple-element.68), channel_id=1, source_target_pairs={{1,0},{0,1},{3,2},{2,3},{5,4},{4,5},{7,6},{6,7},{9,8},{8,9},{11,10... | collective-permute-start | bytes 98312 | tf_op jit(solution)/shard_map/ppermute | solution.py:20
  354.7 7.0 %collective-permute-start.19 = (f32[1,6,6,8,3]{4,3,2,1,0:T(8,128)S(1)}, f32[1,6,6,8,3]{4,3,2,1,0:T(8,128)S(1)}, u32[]{:S(2)}, u32[]{:S(2)}) collective-permute-start(f32[1,6,6,8,3]{4,3,2,1,0:T(8,128)S(1)} %bitcast.118), channel_id=1, source_target_pairs={{16,0},{32,16},{48,32},{64,48},{80,64},{96,80},{112,96},{128,112},... | collective-permute-start | bytes 10376 | tf_op jit(solution)/shard_map/ppermute | solution.py:20
  359.6 9.2 %collective-permute-start.18 = (f32[1,6,6,8,3]{4,3,2,1,0:T(8,128)S(1)}, f32[1,6,6,8,3]{4,3,2,1,0:T(8,128)S(1)}, u32[]{:S(2)}, u32[]{:S(2)}) collective-permute-start(f32[1,6,6,8,3]{4,3,2,1,0:T(8,128)S(1)} %bitcast.116), channel_id=1, source_target_pairs={{0,16},{16,32},{32,48},{48,64},{64,80},{80,96},{96,112},{112,128},... | collective-permute-start | bytes 10376 | tf_op jit(solution)/shard_map/ppermute | solution.py:19
  368.9 8.1 %collective-permute-start.20 = (f32[2,1,6,8,3]{4,3,2,1,0:T(8,128)S(1)}, f32[2,1,6,8,3]{4,3,2,1,0:T(8,128)S(1)}, u32[]{:S(2)}, u32[]{:S(2)}) collective-permute-start(f32[2,1,6,8,3]{4,3,2,1,0:T(8,128)S(1)} %pad_maximum_fusion.24), channel_id=1, source_target_pairs={{0,2},{2,4},{4,6},{6,8},{8,10},{10,12},{12,14},{14,0},{1,3},{3,5},... | collective-permute-start | bytes 3464 | tf_op jit(solution)/shard_map/ppermute | solution.py:19
  377.0 7.4 %collective-permute-start.21 = (f32[2,1,6,8,3]{4,3,2,1,0:T(8,128)S(1)}, f32[2,1,6,8,3]{4,3,2,1,0:T(8,128)S(1)}, u32[]{:S(2)}, u32[]{:S(2)}) collective-permute-start(f32[2,1,6,8,3]{4,3,2,1,0:T(8,128)S(1)} %get-tuple-element.57), channel_id=1, source_target_pairs={{2,0},{4,2},{6,4},{8,6},{10,8},{12,10},{14,12},{0,14},{3,1},{5,3},... | collective-permute-start | bytes 3464 | tf_op jit(solution)/shard_map/ppermute | solution.py:20
  384.4 8.6 %collective-permute-start.22 = (f32[2,4,1,8,3]{4,3,2,1,0:T(8,128)S(1)}, f32[2,4,1,8,3]{4,3,2,1,0:T(8,128)S(1)}, u32[]{:S(2)}, u32[]{:S(2)}) collective-permute-start(f32[2,4,1,8,3]{4,3,2,1,0:T(8,128)S(1)} %pad_maximum_fusion.28), channel_id=1, source_target_pairs={{0,1},{1,0},{2,3},{3,2},{4,5},{5,4},{6,7},{7,6},{8,9},{9,8},{10,11... | collective-permute-start | bytes 2312 | tf_op jit(solution)/shard_map/ppermute | solution.py:19
  392.9 8.6 %collective-permute-start.23 = (f32[2,4,1,8,3]{4,3,2,1,0:T(8,128)S(1)}, f32[2,4,1,8,3]{4,3,2,1,0:T(8,128)S(1)}, u32[]{:S(2)}, u32[]{:S(2)}) collective-permute-start(f32[2,4,1,8,3]{4,3,2,1,0:T(8,128)S(1)} %get-tuple-element.66), channel_id=1, source_target_pairs={{1,0},{0,1},{3,2},{2,3},{5,4},{4,5},{7,6},{6,7},{9,8},{8,9},{11,10... | collective-permute-start | bytes 2312 | tf_op jit(solution)/shard_map/ppermute | solution.py:20
  (49 other events, 734.0 us)
where the time goes:
time: 411 us; the launch traced here: 403 us
  matrix products  128 us (31%)
  starting transfers between devices  108 us (26%)
  other arithmetic  59.3 us (14%)
  local copies, waits for them, and re-layouts  55 us (13%)
  waiting for transfers between devices  49.8 us (12%)
    dot_general x4, matrix products, interact(): jnp.einsum('...k,kc->...c', radial_basis, radial_w, precision=highest)  72 us
    ppermute x12, starting transfers between devices, padded(): before = lax.ppermute(last, axis, up)  55 us
    ppermute x12, starting transfers between devices, padded(): after = lax.ppermute(initial, axis, down)  53.2 us
    ppermute x12, waiting for transfers between devices, padded(): after = lax.ppermute(initial, axis, down)  32.1 us
    dot_general x6, matrix products, interact(): jnp.einsum('...em,...ec->...mc', first_order, term_one, precision=highest)  28.2 us
    gather x2, local copies, waits for them, and re-layouts, layer_apply(): senders = feat_ext.reshape(-1, channels)[sender_idx]  24.8 us
    scatter-add x1, other arithmetic, layer_apply(): senders = feat_ext.reshape(-1, channels)[sender_idx]  23.7 us
    dot_general x6, matrix products, interact(): jnp.einsum('...em,...ec->...mc', second_order, term_two, precision=highest)  23.6 us
  transfers between devices with their start and end apart: 24, of which 15 were waited for; matrix products, arithmetic and copies ran while one was open for 14% of the time, Pallas kernels for 0%

commit v1 on v0

v1 whole, which is shorter than its diff:
```python
import math

import jax
import jax.numpy as jnp
from jax import lax
from jax.experimental import pallas as pl
from jax.experimental.pallas import tpu as pltpu
from jax.sharding import PartitionSpec as P

f32 = jnp.float32
bf16 = jnp.bfloat16
i32 = jnp.int32

E = 16
C = 128
NB = 8
L = 128
CUT = 2.0
GAMMA = ((NB - 1) / CUT) ** 2
SCALE = E**-0.5
R3 = math.sqrt(3.0)
R5 = math.sqrt(5.0)
R15 = math.sqrt(15.0)
VMEM = pltpu.VMEM
SMEM = pltpu.SMEM


def split2(x):
    high = x.astype(bf16)
    low = (x - high.astype(f32)).astype(bf16)
    return high, low


def split3(x):
    high = x.astype(bf16)
    rest = x - high.astype(f32)
    mid = rest.astype(bf16)
    low = (rest - mid.astype(f32)).astype(bf16)
    return high, mid, low


def dot(a, b, dims=((1,), (0,))):
    return lax.dot_general(a, b, (dims, ((), ())), preferred_element_type=f32)


def iota(shape, dim):
    return lax.broadcasted_iota(i32, shape, dim)


def roll(x, shift):
    return pltpu.roll(x, shift % x.shape[-1], x.ndim - 1)


def lanes(shape):
    return iota(shape, len(shape) - 1)


def pack_kernel(gz_ref, pos_ref, spec_ref, nbr_ref, mask_ref, own_ref, straight_ref, cross_ref):
    eye16 = jnp.where(iota((E, E), 0) == iota((E, E), 1), 1.0, 0.0).astype(bf16)
    own_ref[0:16, :] = dot(eye16, nbr_ref[...].astype(f32).astype(bf16), ((1,), (1,)))
    own_ref[16:32, :] = dot(eye16, mask_ref[...].astype(f32).astype(bf16), ((1,), (1,)))
    eye3 = jnp.where(iota((8, 3), 0) == iota((8, 3), 1), 1.0, 0.0).astype(bf16)
    high, mid, low = split3(pos_ref[...])
    nt = ((1,), (1,))
    tail = (dot(eye3, high, nt) + dot(eye3, mid, nt)) + dot(eye3, low, nt)
    lane, slot = iota((8, 256), 1), iota((8, 256), 0)
    total = jnp.zeros((4, 256), f32)
    for i in range(8):
        pick = jnp.where((lane % 8 == slot) & (lane // 32 == i), 1.0, 0.0).astype(bf16)
        total = total + dot(spec_ref[i].astype(f32).astype(bf16), pick)
    keep = (iota((4, 256), 1) // 8) % 4 == iota((4, 256), 0)
    species = jnp.sum(jnp.where(keep, total, 0.0), 0, keepdims=True)
    own_ref[32:40, :] = jnp.where(iota((8, 256), 0) == 3, species, tail)

    lower = lanes((40, L)) < 64
    first, second = own_ref[:, 0:128], own_ref[:, 128:256]
    rows_low = jnp.where(lower, first, roll(second, 64))
    rows_high = jnp.where(lower, roll(first, 64), second)
    front = gz_ref[0] == 0
    straight_ref[...] = jnp.where(front, rows_high, rows_low)
    cross_ref[...] = jnp.where(front, rows_low, rows_high)


def spread(half0, half1, start):
    quarter = lanes((40, L)) // 32
    out = roll(half0, -start)
    out = jnp.where(quarter == 1, roll(half1, 32 - start), out)
    out = jnp.where(quarter == 2, roll(half0, 32 - start), out)
    return jnp.where(quarter == 3, roll(half1, 64 - start), out)


def halves(first, second):
    return roll(jnp.where(lanes(first.shape) >= 64, first, second), 64)


def rows_kernel(gz_ref, all_ref, straight_ref, cross_ref, left_ref, right_ref):
    front = gz_ref[0] == 0
    near0 = jnp.where(front, straight_ref[...], cross_ref[...])
    near1 = jnp.where(front, cross_ref[...], straight_ref[...])
    for x in range(2):
        near = spread(near0, near1, 64 * x)
        own = [
            spread(all_ref[0, :, x * L : (x + 1) * L], all_ref[1, :, x * L : (x + 1) * L], 64 * pair)
            for pair in range(2)
        ]
        tiles = [
            jnp.where(front, near, own[0]),
            jnp.where(front, own[0], own[1]),
            jnp.where(front, own[1], near),
        ]
        for pair in range(3):
            at = (x * 3 + pair) * 4
            left_ref[at : at + 4, :] = tiles[pair][32:36]
            right_ref[at : at + 4, :] = tiles[pair][32:36]
        out = left_ref if x == 0 else right_ref
        for r in range(2):
            out[24 + 32 * r : 56 + 32 * r, :] = halves(tiles[r][0:32], tiles[r + 1][0:32])


def weights_kernel(emb_ref, rad_ref, mix_ref, read_ref, vf_ref, vb_ref, wf_ref, wb_ref, mf_ref, mb_ref, et_ref, ro_ref):
    emb = emb_ref[...]
    for q in range(3):
        base = rad_ref[0, :, q * C : (q + 1) * C] * SCALE
        v = jnp.concatenate([base * emb[k : k + 1] for k in range(4)], 0)
        high, low = split2(v)
        vb_ref[q, 0:32, 0:128] = high
        vb_ref[q, 0:32, 128:256] = high
        vb_ref[q, 32:64, 0:128] = low
        vb_ref[q, 32:64, 128:256] = jnp.zeros((32, 128), bf16)
        vt = v.T
        high, low = split2(vt)
        vf_ref[q] = jnp.concatenate([high.astype(f32), high.astype(f32), low.astype(f32)], 1).astype(bf16)
        w = rad_ref[1, :, q * C : (q + 1) * C]
        high, low = split2(w)
        both = jnp.concatenate([high.astype(f32), low.astype(f32)], 0)
        wb_ref[q, :, 0:128] = both.astype(bf16)
        wb_ref[q, :, 128:256] = jnp.where(iota((16, 128), 0) < 8, both, 0.0).astype(bf16)
        high, low = split2(w.T)
        wf_ref[q * C : (q + 1) * C, :] = jnp.concatenate(
            [high.astype(f32), high.astype(f32), low.astype(f32)], 1
        ).astype(bf16)
    for layer in range(2):
        for q in range(3):
            m = mix_ref[layer, q * C : (q + 1) * C, :]
            high, low = split2(m)
            mb_ref[layer, q * C : (q + 1) * C, 0:128] = high
            mb_ref[layer, q * C : (q + 1) * C, 128:256] = high
            mb_ref[layer, q * C : (q + 1) * C, 256:384] = low
            high, low = split2(m.T)
            mf_ref[layer, :, q * C : (q + 1) * C] = high
            mf_ref[layer, :, 384 + q * C : 384 + (q + 1) * C] = high
            mf_ref[layer, :, 768 + q * C : 768 + (q + 1) * C] = low
    high, mid, low = split3(emb)
    stack = jnp.concatenate([high.astype(f32), mid.astype(f32), low.astype(f32), jnp.zeros((4, C), f32)], 0)
    et_ref[...] = stack.T.astype(bf16)
    ro_ref[...] = jnp.broadcast_to(read_ref[...], (C, L)).T


def decode(ids):
    cell = ids >> 3
    ox = (cell >= 9).astype(i32) + (cell >= 18).astype(i32)
    rest = cell - 9 * ox
    oy = (rest >= 3).astype(i32) + (rest >= 6).astype(i32)
    oz = rest - 3 * oy
    lane = lanes(ids.shape)
    ys = (lane >> 6) + oy
    zs = ((lane >> 3) + oz + 7) & 7
    tile = ox * 2 + (ys >> 1)
    target = ((ys & 1) << 6) | (zs << 3) | (ids & 7)
    return ox, oy, oz, tile, target


PX, PY, PZ, RAD, RINV, UM, TM, SP, TILE, TARGET, Y1X, Y1Y, Y1Z, Y20, Y21, Y22, Y23, Y24 = range(18)
ORDERS = ((Y1X, Y1Y, Y1Z), (Y20, Y21, Y22, Y23, Y24))


def harmonics(geo, at, px, py, pz):
    geo[at, Y1X] = R3 * px
    geo[at, Y1Y] = R3 * py
    geo[at, Y1Z] = R3 * pz
    geo[at, Y20] = R15 * px * py
    geo[at, Y21] = R15 * py * pz
    geo[at, Y22] = (0.5 * R5) * (2.0 * pz * pz - px * px - py * py)
    geo[at, Y23] = R15 * px * pz
    geo[at, Y24] = (0.5 * R15) * (px * px - py * py)


def silu_parts(v):
    gate = 1.0 / (1.0 + jnp.exp(-v))
    return v * gate, gate * (1.0 + v * (1.0 - gate))


def main_kernel(
    off_ref, lown_ref, rown_ref, froml_ref, fromr_ref,
    vf_ref, vb_ref, wf_ref, wb_ref, mf_ref, mb_ref, et_ref, ro_ref,
    outl_ref, outo_ref, outr_ref,
    table, edges, geo, basis, slope, moment, hid, dsilu, dhid, dmom, inv, geo2, rb2, rbst, hg, onehot,
    hs, rad2, efac, dhs, drad, extra, pick, force,
):
    for plane, (ref, base) in enumerate(
        ((froml_ref, 0), (froml_ref, 1), (lown_ref, 0), (lown_ref, 1), (fromr_ref, 0), (fromr_ref, 1))
    ):
        for pair in range(3):
            at = (base * 3 + pair) * 4
            table[plane * 3 + pair, 0:4, :] = ref[at : at + 4, :]
    for plane, ref in enumerate((froml_ref, lown_ref, rown_ref, fromr_ref)):
        for r in range(2):
            edges[plane * 2 + r] = ref[24 + 32 * r : 56 + 32 * r, :]

    centre = iota((NB, L), 0).astype(f32) * (CUT / (NB - 1))
    lane8 = lanes((8, L))

    def layer_one(xr, _):
        kinds = []
        for r in range(2):
            at = xr * 2 + r
            own_a = table[(xr + 1) * 3 + r]
            own_b = table[(xr + 1) * 3 + r + 1]
            own = halves(own_a, own_b)
            kinds.append(own[3:4])
            ids = edges[at, 0:16, :].astype(i32)
            ox, oy, oz, tile, target = decode(ids)
            got = [jnp.zeros((E, L), f32) for _ in range(4)]
            for t in range(6):
                src = table[(xr + t // 2) * 3 + r + t % 2]
                here = tile == t
                for q in range(4):
                    wide = jnp.broadcast_to(src[q : q + 1], (E, L))
                    val = jnp.take_along_axis(wide, target, axis=1, mode="promise_in_bounds")
                    got[q] = jnp.where(here, val, got[q])
            dx = ((ox - 1).astype(f32) + got[0]) - own[0:1]
            dy = ((oy - 1).astype(f32) + got[1]) - own[1:2]
            dz = ((oz - 1).astype(f32) + got[2]) - own[2:3]
            sq = dx * dx + dy * dy + dz * dz
            rinv = lax.rsqrt(sq)
            dist = jnp.sqrt(sq)
            mask = edges[at, 16:32, :]
            part = jnp.where(dist < CUT, 1.0 - sq * (1.0 / CUT**2), 0.0) * mask
            px, py, pz = 0.5 * dx, 0.5 * dy, 0.5 * dz
            geo[at, PX] = px
            geo[at, PY] = py
            geo[at, PZ] = pz
            geo[at, RAD] = dist
            geo[at, RINV] = rinv
            geo[at, UM] = part * part
            geo[at, TM] = part
            geo[at, SP] = got[3]
            geo[at, TILE] = tile.astype(f32)
            geo[at, TARGET] = target.astype(f32)
            harmonics(geo, at, px, py, pz)

            acc = [[None] * 4 for _ in range(9)]
            for e in range(E):
                def row(i):
                    return jnp.broadcast_to(geo[at, i, e : e + 1, :], (NB, L))

                diff = row(RAD) - centre
                bump = jnp.exp(-GAMMA * (diff * diff))
                rb = bump * row(UM)
                basis[at, e * 8 : e * 8 + 8, :] = rb
                slope[at, e * 8 : e * 8 + 8, :] = -(bump * row(TM)) - (2.0 * GAMMA) * (diff * rb * row(RINV))
                kind = row(SP)
                per = [jnp.where(kind == float(k), rb, 0.0) for k in range(4)]
                for qm in range(9):
                    y = None if qm == 0 else row(Y1X + qm - 1)
                    for k in range(4):
                        term = per[k] if y is None else y * per[k]
                        acc[qm][k] = term if e == 0 else acc[qm][k] + term
            first = 0
            for q, count in enumerate((1, 3, 5)):
                blocks = []
                for m in range(count):
                    p = jnp.concatenate(acc[first + m], 0)
                    high, low = split2(p)
                    blocks.append(jnp.concatenate([high, low, high], 0))
                first += count
                out = dot(vf_ref[q], jnp.concatenate(blocks, 1) if count > 1 else blocks[0])
                if q == 0:
                    value = out
                else:
                    value = None
                    for m in range(count):
                        a = out[:, m * L : (m + 1) * L]
                        moment[at, (0, 3)[q - 1] + m] = a
                        value = a * a if value is None else value + a * a
                high, low = split2(value)
                inv[q * C : (q + 1) * C, r * L : (r + 1) * L] = high
                inv[384 + q * C : 384 + (q + 1) * C, r * L : (r + 1) * L] = low
                inv[768 + q * C : 768 + (q + 1) * C, r * L : (r + 1) * L] = high
        z = dot(mf_ref[0], inv[...])
        update, slope_z = silu_parts(z)
        kind = jnp.concatenate([jnp.broadcast_to(k, (16, L)) for k in kinds], 1)
        sel = iota((16, 2 * L), 0)
        hot = jnp.where((kind == (sel % 4).astype(f32)) & (sel < 12), 1.0, 0.0).astype(bf16)
        h1 = dot(et_ref[...], hot) + update
        for r in range(2):
            hid[xr * 2 + r] = h1[:, r * L : (r + 1) * L]
            dsilu[xr * 2 + r] = slope_z[:, r * L : (r + 1) * L]
        return 0

    lax.fori_loop(0, 4, layer_one, 0)

    read = ro_ref[...]
    low_half = lanes((C, L)) < 64
    for plane in range(4):
        for r in range(2):
            if plane in (1, 2):
                keep = low_half if r == 1 else ~low_half
                dhid[plane * 2 + r] = jnp.where(keep, read, 0.0)
            else:
                dhid[plane * 2 + r] = jnp.zeros((C, L), f32)

    def layer_two(x, _):
        a, b = (x + 1) * 2, (x + 1) * 2 + 1
        ids = halves(edges[a, 0:16, :], edges[b, 0:16, :]).astype(i32)
        _, _, _, tile, target = decode(ids)
        geo2[TILE] = tile.astype(f32)
        geo2[TARGET] = target.astype(f32)
        for i in (PX, PY, PZ, Y1X, Y1Y, Y1Z, Y20, Y21, Y22, Y23, Y24):
            geo2[i] = halves(geo[a, i], geo[b, i])
        rb2[...] = halves(basis[a], basis[b])
        for e in range(E):
            high, low = split2(rb2[e * 8 : e * 8 + 8, :])
            high = high.astype(f32)
            rbst[:, e * L : (e + 1) * L] = jnp.concatenate([high, low.astype(f32), high], 0).astype(bf16)
        for t in range(6):
            h = hid[(x + t // 2) * 2 + t % 2]
            high, low = split2(h)
            hg[0:128, t * L : (t + 1) * L] = high
            hg[128:256, t * L : (t + 1) * L] = low
        spot = iota((C, L), 0).astype(f32).astype(bf16)
        one, zero = jnp.ones((), bf16), jnp.zeros((), bf16)
        for e in range(E):
            where_t = geo2[TILE, e : e + 1, :]
            where_l = geo2[TARGET, e : e + 1, :]
            for t in range(6):
                code = jnp.where(where_t == float(t), where_l, -1.0).astype(bf16)
                hot = jnp.where(spot == jnp.broadcast_to(code, (C, L)), one, zero)
                onehot[t * L : (t + 1) * L, e * L : (e + 1) * L] = hot

        def gather(i, _):
            at = pl.ds(pl.multiple_of(i * 256, 256), 256)
            out = dot(hg[...], onehot[:, at])
            hs[:, at] = out[0:128] + out[128:256]
            rad2[:, at] = dot(wf_ref[...], rbst[:, at])
            return 0

        lax.fori_loop(0, 8, gather, 0)

        def contract(i, _):
            rows = pl.multiple_of(i * 16, 16)
            acc = [None] * 9
            for e in range(E):
                cols = slice(e * L, (e + 1) * L)
                h = hs[pl.ds(rows, 16), cols]
                ts = [rad2[pl.ds(q * C + rows, 16), cols] * h for q in range(3)]
                for qm in range(9):
                    if qm == 0:
                        term = ts[0]
                    else:
                        y = jnp.broadcast_to(geo2[Y1X + qm - 1, e : e + 1, :], (16, L))
                        term = y * ts[1 if qm < 4 else 2]
                    acc[qm] = term if e == 0 else acc[qm] + term
            for qm in range(9):
                efac[qm, pl.ds(rows, 16), :] = acc[qm] * SCALE
            return 0

        lax.fori_loop(0, 8, contract, 0)

        one_sq = efac[1] * efac[1] + efac[2] * efac[2] + efac[3] * efac[3]
        two_sq = efac[4] * efac[4]
        for m in range(5, 9):
            two_sq = two_sq + efac[m] * efac[m]
        for q, value in enumerate((efac[0], one_sq, two_sq)):
            high, low = split2(value)
            inv[q * C : (q + 1) * C, 0:128] = high
            inv[384 + q * C : 384 + (q + 1) * C, 0:128] = low
            inv[768 + q * C : 768 + (q + 1) * C, 0:128] = high
        z = dot(mf_ref[1], inv[:, 0:128])
        update, slope_z = silu_parts(z)
        h2 = halves(hid[a], hid[b]) + update
        kind = table[(x + 2) * 3 + 1, 3:4, :]
        offset = jnp.zeros((1, L), f32)
        for k in range(4):
            offset = jnp.where(kind == float(k), off_ref[k], offset)
        energy = jnp.sum(read * h2, 0, keepdims=True) + offset
        geo2[RAD, 0:1, :] = energy
        extra[x, 0, 0, 0:1, :] = energy

        high, low = split2(read * slope_z)
        dinv = dot(mb_ref[1], jnp.concatenate([high, low, high], 0))
        efac[0] = dinv[0:128] * SCALE
        for m in range(1, 9):
            part = dinv[128:256] if m < 4 else dinv[256:384]
            efac[m] = efac[m] * part * (2.0 * SCALE)

        def back(e, _):
            cols = pl.ds(pl.multiple_of(e * L, L), L)

            def row(i):
                return jnp.broadcast_to(geo2[i, pl.ds(e, 1), :], (16, L))

            ys = [None] + [row(Y1X + m) for m in range(8)]
            acc = [None] * 9
            for i in range(8):
                rows = slice(i * 16, i * 16 + 16)
                h = hs[rows, cols]
                rr = [rad2[q * C + i * 16 : q * C + i * 16 + 16, cols] for q in range(3)]
                ef = [efac[qm, rows, :] for qm in range(9)]
                d0 = ef[0]
                d1 = ys[1] * ef[1] + ys[2] * ef[2] + ys[3] * ef[3]
                d2 = ys[4] * ef[4] + ys[5] * ef[5] + ys[6] * ef[6] + ys[7] * ef[7] + ys[8] * ef[8]
                t1 = rr[1] * h
                t2 = rr[2] * h
                for qm in range(1, 9):
                    term = (t1 if qm < 4 else t2) * ef[qm]
                    acc[qm] = term if i == 0 else acc[qm] + term
                high, low = split2(d0 * rr[0] + d1 * rr[1] + d2 * rr[2])
                dhs[rows, cols] = high
                dhs[128 + i * 16 : 144 + i * 16, cols] = low
                for q, d in enumerate((d0, d1, d2)):
                    high, low = split2(d * h)
                    drad[q, rows, cols] = high
                    drad[q, 128 + i * 16 : 144 + i * 16, cols] = low
            fold = [None] + [acc[m][0:8] + acc[m][8:16] for m in range(1, 9)]
            px, py, pz = (jnp.broadcast_to(geo2[i, pl.ds(e, 1), :], (8, L)) for i in (PX, PY, PZ))
            gx = R3 * fold[1] + R15 * (py * fold[4] + pz * fold[7] + px * fold[8]) - R5 * (px * fold[6])
            gy = R3 * fold[2] + R15 * (px * fold[4] + pz * fold[5] - py * fold[8]) - R5 * (py * fold[6])
            gz = R3 * fold[3] + R15 * (py * fold[5] + px * fold[7]) + (2.0 * R5) * (pz * fold[6])
            extra[x, e + 1, 1] = roll(0.5 * gx, 64)
            extra[x, e + 1, 2] = roll(0.5 * gy, 64)
            extra[x, e + 1, 3] = roll(0.5 * gz, 64)
            return 0

        lax.fori_loop(0, E, back, 0)

        grad = dot(wb_ref[0], drad[0]) + dot(wb_ref[1], drad[1]) + dot(wb_ref[2], drad[2])
        for e in range(E):
            g = grad[0:8, e * L : (e + 1) * L] + grad[8:16, e * L : (e + 1) * L]
            extra[x, e + 1, 0] = roll(g, 64)
        for t in range(6):
            out = dot(dhs[...], onehot[t * L : (t + 1) * L, :], ((1,), (1,)))
            at = (x + t // 2) * 2 + t % 2
            dhid[at] = dhid[at] + (out[0:128] + out[128:256])
        return 0

    lax.fori_loop(0, 2, layer_two, 0)

    for i in range(18):
        force[i] = jnp.zeros((8, L), f32)
    sub8 = iota((8, L), 0)
    spot = iota((C, L), 0).astype(f32).astype(bf16)
    one, zero = jnp.ones((), bf16), jnp.zeros((), bf16)

    def layer_one_back(xr, _):
        inner = (xr == 1) | (xr == 2)
        x_own = jnp.clip(xr - 1, 0, 1)
        dz = jnp.concatenate([dhid[xr * 2 + r] * dsilu[xr * 2 + r] for r in range(2)], 1)
        high, low = split2(dz)
        dinv = dot(mb_ref[0], jnp.concatenate([high, low, high], 0))
        for r in range(2):
            at = xr * 2 + r
            cols = slice(r * L, (r + 1) * L)
            first = 0
            for q, count in enumerate((1, 3, 5)):
                part = dinv[q * C : (q + 1) * C, cols]
                blocks = []
                for m in range(count):
                    da = part if q == 0 else 2.0 * moment[at, (0, 3)[q - 1] + m] * part
                    high, low = split2(da)
                    blocks.append(jnp.concatenate([high, low], 0))
                out = dot(vb_ref[q], jnp.concatenate(blocks, 1) if count > 1 else blocks[0])
                for m in range(count):
                    one_m = out[:, m * L : (m + 1) * L]
                    dmom[first + m] = one_m[0:32] + one_m[32:64]
                first += count
            keep = ((lane8 >= 64) if r == 0 else (lane8 < 64)) & inner
            received = jnp.zeros((8, L), f32)
            for e in range(E):
                def row(i):
                    return jnp.broadcast_to(geo[at, i, e : e + 1, :], (NB, L))

                kind = row(SP)
                is0, is1, is2 = kind == 0.0, kind == 1.0, kind == 2.0
                dp = []
                for qm in range(9):
                    sel = jnp.where(is2, dmom[qm, 16:24, :], dmom[qm, 24:32, :])
                    sel = jnp.where(is1, dmom[qm, 8:16, :], sel)
                    dp.append(jnp.where(is0, dmom[qm, 0:8, :], sel))
                rb = basis[at, e * 8 : e * 8 + 8, :]
                g = dp[0]
                for m in range(8):
                    g = g + row(Y1X + m) * dp[m + 1]
                g = g + jnp.where(keep, extra[x_own, e + 1, 0], 0.0)
                radial = (2.0 * g) * slope[at, e * 8 : e * 8 + 8, :]
                px, py, pz = row(PX), row(PY), row(PZ)
                c22 = dp[6] * (1.0 / R3)
                half = (0.5 * R15) * rb
                hr = (0.5 * R3) * rb
                gx = px * radial + hr * dp[1] + half * (py * dp[4] + pz * dp[7] + px * (dp[8] - c22))
                gy = py * radial + hr * dp[2] + half * (px * dp[4] + pz * dp[5] - py * (dp[8] + c22))
                gz = pz * radial + hr * dp[3] + half * (py * dp[5] + px * dp[7] + pz * (c22 + c22))
                gx = gx + jnp.where(keep, extra[x_own, e + 1, 1], 0.0)
                gy = gy + jnp.where(keep, extra[x_own, e + 1, 2], 0.0)
                gz = gz + jnp.where(keep, extra[x_own, e + 1, 3], 0.0)
                sx = jnp.sum(gx, 0, keepdims=True)
                sy = jnp.sum(gy, 0, keepdims=True)
                sz = jnp.sum(gz, 0, keepdims=True)
                vec = jnp.where(sub8 == 0, sx, jnp.where(sub8 == 1, sy, jnp.where(sub8 == 2, sz, 0.0)))
                received = received + vec
                high, low = split2(vec)
                both = jnp.concatenate([high.astype(f32), low.astype(f32)], 0)
                where_t = jnp.broadcast_to(geo[at, TILE, e : e + 1, :], (16, L))
                for t in range(6):
                    pick[t * 16 : (t + 1) * 16, e * L : (e + 1) * L] = jnp.where(
                        where_t == float(t), both, 0.0
                    ).astype(bf16)
                code = jnp.broadcast_to(geo[at, TARGET, e : e + 1, :].astype(bf16), (C, L))
                onehot[0:128, e * L : (e + 1) * L] = jnp.where(spot == code, one, zero)
            sent = dot(pick[...], onehot[0:128, :], ((1,), (1,)))
            for t in range(6):
                to = (xr + t // 2) * 3 + r + t % 2
                force[to] = force[to] - (sent[t * 16 : t * 16 + 8] + sent[t * 16 + 8 : t * 16 + 16])
            turned = roll(received, 64)
            mine = (xr + 1) * 3 + r
            force[mine] = force[mine] + jnp.where(lane8 >= 64, turned, 0.0)
            force[mine + 1] = force[mine + 1] + jnp.where(lane8 < 64, turned, 0.0)
        return 0

    lax.fori_loop(0, 4, layer_one_back, 0)

    for plane in range(6):
        for pair in range(3):
            out = (outl_ref, outo_ref, outr_ref)[plane // 2]
            at = ((plane % 2) * 3 + pair) * 4
            out[at : at + 4, :] = force[plane * 3 + pair, 0:4, :]
            if plane in (2, 3) and pair == 1:
                out[at + 3 : at + 4, :] = extra[plane - 2, 0, 0, 0:1, :]


def chunk_kernel(place_ref, own_ref, left_ref, right_ref, out_ref):
    gy, gz = place_ref[0], place_ref[1]
    front = gz == 0
    total = own_ref[...] + left_ref[...] + right_ref[...]
    quarter = lanes((4, L)) // 32

    def squeeze(pair, zh):
        first = total[pair * 4 : pair * 4 + 4]
        second = total[12 + pair * 4 : 16 + pair * 4]
        out = roll(first, -32 * zh)
        out = jnp.where(quarter == 1, roll(first, -32 - 32 * zh), out)
        out = jnp.where(quarter == 2, roll(second, 64 - 32 * zh), out)
        return jnp.where(quarter == 3, roll(second, 32 - 32 * zh), out)

    out_ref[...] = jnp.zeros(out_ref.shape, f32)
    y_count = out_ref.shape[0] // 2
    beside = jnp.where(front, gy + y_count - 1, gy + 1)
    beside = jnp.where(beside >= y_count, beside - y_count, beside)
    for zh in range(2):
        parts = [squeeze(pair, zh) for pair in range(3)]
        low = jnp.where(front, parts[1], parts[0])
        high = jnp.where(front, parts[2], parts[1])
        near = jnp.where(front, parts[0], parts[2])
        out_ref[gy * 2 + zh] = jnp.concatenate([low, high], 0)
        out_ref[beside * 2 + zh, 0:4, :] = near


def unpack_kernel(place_ref, got_ref, energy_ref, force_ref):
    gy = place_ref[0]
    y_count = got_ref.shape[0] // 2
    below = jnp.where(gy == 0, y_count - 1, gy - 1)
    above = jnp.where(gy == y_count - 1, 0, gy + 1)
    own = got_ref[gy * 2] + got_ref[gy * 2 + 1]
    low = own[0:4] + got_ref[below * 2 + 1, 0:4, :]
    high = own[4:8] + got_ref[above * 2, 0:4, :]
    lower = lanes((4, L)) < 64
    first = jnp.where(lower, low, roll(high, 64))
    second = jnp.where(lower, roll(low, 64), high)
    rows = jnp.concatenate([first, second], 1)
    rows8 = jnp.concatenate([rows, jnp.zeros((4, 256), f32)], 0)
    force_ref[...] = rows8.T[:, 0:3]
    pick = jnp.where(iota((8, 256), 1) % 8 == iota((8, 256), 0), 1.0, 0.0).astype(bf16)
    high, mid, low = split3(rows[3:4])
    lane, cell = iota((4, 256), 1), iota((4, 256), 0)
    nt = ((1,), (1,))
    for i in range(8):
        keep = lane // 8 == cell + 4 * i
        total = None
        for part in (high, mid, low):
            piece = dot(jnp.where(keep, part.astype(f32), 0.0).astype(bf16), pick, nt)
            total = piece if total is None else total + piece
        energy_ref[i] = total


def call(kernel, outs, in_specs, scratch=(), flops=10**6):
    return pl.pallas_call(
        kernel,
        out_shape=outs,
        in_specs=in_specs,
        out_specs=jax.tree.map(lambda _: pl.BlockSpec(memory_space=VMEM), outs),
        scratch_shapes=list(scratch),
        compiler_params=pltpu.CompilerParams(vmem_limit_bytes=60 * 2**20),
        cost_estimate=pl.CostEstimate(flops=flops, bytes_accessed=10**5, transcendentals=0),
    )


def shape(*dims, dtype=f32):
    return jax.ShapeDtypeStruct(dims, dtype)


def shards(
    positions, species, neighbors, edge_mask, species_embed, radial_weight, mix_weight, readout, energy_offset
):
    v = pl.BlockSpec(memory_space=VMEM)
    sm = pl.BlockSpec(memory_space=SMEM)
    gy_count, gz_count = lax.axis_size("gy"), lax.axis_size("gz")
    gx_count = lax.axis_size("gx")
    gy, gz = lax.axis_index("gy"), lax.axis_index("gz")
    place = jnp.stack([gy, gz]).astype(i32)
    gz_only = gz.astype(i32).reshape(1)

    own, straight, cross = call(
        pack_kernel, [shape(40, 256), shape(40, L), shape(40, L)], [sm, v, v, v, v]
    )(
        gz_only,
        positions.reshape(256, 3),
        species.reshape(8, 4, 8),
        neighbors.reshape(256, E),
        edge_mask.reshape(256, E),
    )

    def dev(y, s):
        return (y % gy_count) * gz_count + s

    yz = ("gy", "gz")
    go_straight = [(dev(y, s), dev(y + 1 if s == 0 else y - 1, s)) for y in range(gy_count) for s in range(2)]
    go_cross = [(dev(y, s), dev(y - 1 if s == 0 else y + 1, 1 - s)) for y in range(gy_count) for s in range(2)]
    near_straight = lax.ppermute(straight, yz, go_straight)
    near_cross = lax.ppermute(cross, yz, go_cross)
    both = lax.all_gather(own, "gz")

    left, right = call(rows_kernel, [shape(88, L), shape(88, L)], [sm, v, v, v])(
        gz_only, both, near_straight, near_cross
    )
    up = [(i, (i + 1) % gx_count) for i in range(gx_count)]
    down = [(j, i) for i, j in up]
    from_left = lax.ppermute(right, "gx", up)
    from_right = lax.ppermute(left, "gx", down)

    weights = call(
        weights_kernel,
        [
            shape(3, C, 96, dtype=bf16),
            shape(3, 64, 256, dtype=bf16),
            shape(384, 24, dtype=bf16),
            shape(3, 16, 256, dtype=bf16),
            shape(2, C, 1152, dtype=bf16),
            shape(2, 384, 384, dtype=bf16),
            shape(C, 16, dtype=bf16),
            shape(C, L),
        ],
        [v, v, v, v],
        flops=10**7,
    )(species_embed, radial_weight, mix_weight, readout.reshape(1, C))

    scratch = [
        VMEM((18, 8, L), f32),
        VMEM((8, 32, L), f32),
        VMEM((8, 18, E, L), f32),
        VMEM((8, 128, L), f32),
        VMEM((8, 128, L), f32),
        VMEM((8, 8, C, L), f32),
        VMEM((8, C, L), f32),
        VMEM((8, C, L), f32),
        VMEM((8, C, L), f32),
        VMEM((9, 32, L), f32),
        VMEM((1152, 256), bf16),
        VMEM((18, E, L), f32),
        VMEM((128, L), f32),
        VMEM((24, E * L), bf16),
        VMEM((256, 768), bf16),
        VMEM((768, E * L), bf16),
        VMEM((C, E * L), f32),
        VMEM((384, E * L), f32),
        VMEM((9, C, L), f32),
        VMEM((256, E * L), bf16),
        VMEM((3, 256, E * L), bf16),
        VMEM((2, E + 1, 4, 8, L), f32),
        VMEM((96, E * L), bf16),
        VMEM((18, 8, L), f32),
    ]
    out_left, out_own, out_right = call(
        main_kernel, [shape(24, L)] * 3, [sm] + [v] * 12, scratch, flops=10**9
    )(energy_offset, left, right, from_left, from_right, *weights)

    back_right = lax.ppermute(out_left, "gx", down)
    back_left = lax.ppermute(out_right, "gx", up)
    chunks = call(chunk_kernel, shape(gy_count * 2, 8, L), [sm, v, v, v])(place, out_own, back_left, back_right)
    got = lax.all_to_all(chunks, yz, 0, 0)
    energy, force = call(unpack_kernel, [shape(8, 4, 8), shape(256, 3)], [sm, v])(place, got)
    return energy.reshape(2, 4, 4, 8), force.reshape(2, 4, 4, 8, 3)


def solution(mesh):
    in_specs = (
        P("gx", "gy", "gz", None, None),
        P("gx", "gy", "gz", None),
        P("gx", "gy", "gz", None, None),
        P("gx", "gy", "gz", None, None),
        P(),
        P(),
        P(),
        P(),
        P(),
    )
    out_specs = (P("gx", "gy", "gz", None), P("gx", "gy", "gz", None, None))
    return jax.shard_map(shards, mesh=mesh, in_specs=in_specs, out_specs=out_specs, check_vma=False)
```

time: 411 us -> 112 us (0.27); the launches traced: 403 us -> 112 us
  matrix products: 128 us -> 0 us
  starting transfers between devices: 108 us -> 33.7 us
  other arithmetic: 59.3 us -> 0.67 us
  local copies, waits for them, and re-layouts: 55 us -> 5.3 us
  waiting for transfers between devices: 49.8 us -> 4.63 us
  Pallas kernels: 0 us -> 43.2 us
  blocking collectives: 0 us -> 23.3 us
    dot_general x21 -> x0, matrix products: 128 us -> none  [the longest x4 72 us: interact(): jnp.einsum('...k,kc->...c', radial_basis, radial_w, precision=highest)]
    ppermute x24 -> x6, starting transfers between devices: 108 us -> 33.7 us  [the longest x1 12.1 us: shards(): from_right = lax.ppermute(left, 'gx', down)]
    scatter-add x2 -> x0, other arithmetic: 46.3 us -> none  [the longest x1 23.7 us: layer_apply(): senders = feat_ext.reshape(-1, channels)[sender_idx]]
    gather x7 -> x0, local copies, waits for them, and re-layouts: 45.6 us -> none  [the longest x2 24.8 us: layer_apply(): senders = feat_ext.reshape(-1, channels)[sender_idx]]
    ppermute x24 -> x6, waiting for transfers between devices: 49.8 us -> 4.63 us  [the longest x1 4.27 us: shards(): from_left = lax.ppermute(right, 'gx', up)]
    pallas_call x0 -> x6, Pallas kernels: none -> 43.2 us  [the longest x1 33.7 us: shards(): call(main_kernel, [shape(24, L)] * 3, [sm] + [v] * 12, scratch, flops=10...]
    all_to_all x0 -> x1, blocking collectives: none -> 14.8 us  [shards(): got = lax.all_to_all(chunks, yz, 0, 0)]
    all_gather x0 -> x1, blocking collectives: none -> 8.45 us  [shards(): both = lax.all_gather(own, 'gz')]
  transfers between devices with their start and end apart: 24 -> 6, of which waited for: 15 -> 2; matrix products, arithmetic and copies ran while one was open for 14% -> 1% of each run, Pallas kernels for 0% -> 2%
where the time goes in v1:
time: 112 us
  Pallas kernels  43.2 us (39%)
  starting transfers between devices  33.7 us (30%)
  blocking collectives  23.3 us (21%)
  local copies, waits for them, and re-layouts  5.3 us (5%)
  waiting for transfers between devices  4.63 us (4%)
    pallas_call x1, Pallas kernels, shards(): call(main_kernel, [shape(24, L)] * 3, [sm] + [v] * 12, scratch, flops=10...  33.7 us
    all_to_all x1, blocking collectives, shards(): got = lax.all_to_all(chunks, yz, 0, 0)  14.8 us
    ppermute x1, starting transfers between devices, shards(): from_right = lax.ppermute(left, 'gx', down)  12.1 us
    all_gather x1, blocking collectives, shards(): both = lax.all_gather(own, 'gz')  8.45 us
    ppermute x1, starting transfers between devices, shards(): back_right = lax.ppermute(out_left, 'gx', down)  6.68 us
    ppermute x1, starting transfers between devices, shards(): near_cross = lax.ppermute(cross, yz, go_cross)  6.5 us
    unnamed x14, local copies, waits for them, and re-layouts  5.3 us
    ppermute x1, starting transfers between devices, shards(): near_straight = lax.ppermute(straight, yz, go_straight)  4.58 us
  transfers between devices with their start and end apart: 6, of which 2 were waited for; matrix products, arithmetic and copies ran while one was open for 1% of the time, Pallas kernels for 2%

profile of v1, /device:TPU:1, one launch (start us, length us, event | category | flops | bytes accessed | tf_op | source)
XLA Modules:
  0.0 111.5 jit_solution(10352323254180520910)
XLA Ops:
  0.6 1.7 %copy.11 = f32[2,4,4,8,3]{4,3,2,1,0:T(8,128)} copy(f32[2,4,4,8,3]{3,2,4,1,0:T(4,128)} %param.9) | data formatting | bytes 6144 | tf_op args[0]
  2.3 2.0 %shard_map.104 = (f32[40,256]{1,0:T(8,128)}, f32[40,128]{1,0:T(8,128)}, f32[40,128]{1,0:T(8,128)}) custom-call(s32[1]{0:T(128)} %bitcast.1.gz_ref, f32[256,3]{1,0:T(8,128)} %bitcast.10, s32[8,4,8]{2,1,0:T(4,128)} %bitcast.15, s32[256,16]{1,0:T(8,128)} %bitcast.12, s32[256,16]{1,0:T(8,128)} %bitcast.13), custom_call_target="tpu_custom_call" | custom-call | flops 1000000 | bytes 100000 | tf_op jit(solution)/shard_map/pallas_call | solution.py:622
  4.3 4.6 %collective-permute-start = (f32[40,128]{1,0:T(8,128)}, f32[40,128]{1,0:T(8,128)S(1)}, u32[]{:S(2)}, u32[]{:S(2)}) collective-permute-start(f32[40,128]{1,0:T(8,128)} %get-tuple-element.21), channel_id=1, source_target_pairs={{0,2},{1,15},{2,4},{3,1},{4,6},{5,3},{6,8},{7,5},{8,10},{9,7},{10,... | collective-permute-start | bytes 61448 | tf_op jit(solution)/shard_map/ppermute | solution.py:638
  8.9 6.5 %collective-permute-start.1 = (f32[40,128]{1,0:T(8,128)}, f32[40,128]{1,0:T(8,128)S(1)}, u32[]{:S(2)}, u32[]{:S(2)}) collective-permute-start(f32[40,128]{1,0:T(8,128)} %get-tuple-element.22), channel_id=1, source_target_pairs={{0,15},{1,2},{2,1},{3,4},{4,3},{5,6},{6,5},{7,8},{8,7},{9,10},{10,... | collective-permute-start | bytes 61448 | tf_op jit(solution)/shard_map/ppermute | solution.py:639
  15.4 8.4 %all-gather = f32[80,256]{1,0:T(8,128)} all-gather(f32[40,256]{1,0:T(8,128)} %get-tuple-element.20), channel_id=2, replica_groups=mesh['gx'=32,'gy'=8,'gz'=2] {'gz'}, dimensions={0}, use_global_device_ids=true | all-gather | bytes 122880 | tf_op jit(solution)/shard_map/all_gather | solution.py:640
  23.9 0.6 copy-done
  24.5 1.7 %shard_map.105 = (f32[88,128]{1,0:T(8,128)}, f32[88,128]{1,0:T(8,128)}) custom-call(s32[1]{0:T(128)} %bitcast.1.gz_ref, f32[2,40,256]{2,1,0:T(8,128)} %bitcast.11, f32[40,128]{1,0:T(8,128)} %copy-done, f32[40,128]{1,0:T(8,128)} %copy-done.1), custom_call_target="tpu_custom_call" | custom-call | flops 1000000 | bytes 100000 | tf_op jit(solution)/shard_map/pallas_call | solution.py:642
  26.2 12.1 %collective-permute-start.3 = (f32[88,128]{1,0:T(8,128)}, f32[88,128]{1,0:T(8,128)S(1)}, u32[]{:S(2)}, u32[]{:S(2)}) collective-permute-start(f32[88,128]{1,0:T(8,128)} %get-tuple-element.23.lown_ref), channel_id=1, source_target_pairs={{16,0},{32,16},{48,32},{64,48},{80,64},{96,80},{112,96},{128,112},... | collective-permute-start | bytes 135176 | tf_op jit(solution)/shard_map/ppermute | solution.py:648
  38.4 1.9 %collective-permute-start.2 = (f32[88,128]{1,0:T(8,128)}, f32[88,128]{1,0:T(8,128)S(1)}, u32[]{:S(2)}, u32[]{:S(2)}) collective-permute-start(f32[88,128]{1,0:T(8,128)} %get-tuple-element.24.rown_ref), channel_id=1, source_target_pairs={{0,16},{16,32},{32,48},{48,64},{64,80},{80,96},{96,112},{112,128},... | collective-permute-start | bytes 135176 | tf_op jit(solution)/shard_map/ppermute | solution.py:647
  40.3 2.6 %shard_map.106 = (bf16[3,128,96]{2,1,0:T(8,128)(2,1)}, bf16[3,64,256]{2,1,0:T(8,128)(2,1)}, bf16[384,24]{1,0:T(8,128)(2,1)}, bf16[3,16,256]{2,1,0:T(8,128)(2,1)}...) custom-call(f32[4,128]{1,0:T(4,128)} %emb_ref.1, ...), custom_call_target="tpu_custom_call" | custom-call | flops 10000000 | bytes 100000 | tf_op jit(solution)/shard_map/pallas_call | solution.py:650
  42.9 0.0 collective-permute-done.3.fromr_ref
  42.9 4.3 %collective-permute-done.2.froml_ref = f32[88,128]{1,0:T(8,128)S(1)} collective-permute-done((f32[88,128]{1,0:T(8,128)}, f32[88,128]{1,0:T(8,128)S(1)}, u32[]{:S(2)}, u32[]{:S(2)}) %collective-permute-start.2) | collective-permute-done | bytes 45088 | tf_op jit(solution)/shard_map/ppermute | solution.py:647
  47.1 0.6 copy-done.5
  47.7 33.7 %shard_map.107 = (f32[24,128]{1,0:T(8,128)}, f32[24,128]{1,0:T(8,128)}, f32[24,128]{1,0:T(8,128)}) custom-call(f32[4]{0:T(128)} %off_ref.1, f32[88,128]{1,0:T(8,128)} %get-tuple-element.23.lown_ref, f32[88,128]{1,0:T(8,128)} %get-tuple-element.24.rown_ref, f32[88,128]{1,0:T(8,128)} %copy-done.5, f32[88,128]{1,0:T(8,128)} %copy-done.4, ...), custom_call_target="tpu_custom_call" | custom-call | flops 1000000000 | bytes 100000 | tf_op jit(solution)/shard_map/pallas_call | solution.py:692
  81.4 1.9 %collective-permute-start.4 = (f32[24,128]{1,0:T(8,128)}, f32[24,128]{1,0:T(8,128)S(1)}, u32[]{:S(2)}, u32[]{:S(2)}) collective-permute-start(f32[24,128]{1,0:T(8,128)} %get-tuple-element.34), channel_id=1, source_target_pairs={{0,16},{16,32},{32,48},{48,64},{64,80},{80,96},{96,112},{112,128},... | collective-permute-start | bytes 36872 | tf_op jit(solution)/shard_map/ppermute | solution.py:697
  83.3 6.7 %collective-permute-start.5 = (f32[24,128]{1,0:T(8,128)}, f32[24,128]{1,0:T(8,128)S(1)}, u32[]{:S(2)}, u32[]{:S(2)}) collective-permute-start(f32[24,128]{1,0:T(8,128)} %get-tuple-element.35), channel_id=1, source_target_pairs={{16,0},{32,16},{48,32},{64,48},{80,64},{96,80},{112,96},{128,112},... | collective-permute-start | bytes 36872 | tf_op jit(solution)/shard_map/ppermute | solution.py:696
  90.0 0.7 pad_add_fusion.place_ref
  90.7 0.3 collective-permute-done.5.right_ref
  91.1 0.2 copy-done.2
  91.3 0.3 copy-done.3
  91.7 1.5 %shard_map.108 = f32[16,8,128]{2,1,0:T(8,128)} custom-call(s32[2]{0:T(128)} %pad_add_fusion.place_ref, f32[24,128]{1,0:T(8,128)} %get-tuple-element.33.own_ref, f32[24,128]{1,0:T(8,128)} %copy-done.2, f32[24,128]{1,0:T(8,128)} %copy-done.3), custom_call_target="tpu_custom_call" | custom-call | flops 1000000 | bytes 100000 | tf_op jit(solution)/shard_map/pallas_call | solution.py:698
  93.2 14.8 %all_to_all.5.got_ref = f32[16,8,128]{2,1,0:T(8,128)} all-to-all(f32[16,8,128]{2,1,0:T(8,128)} %shard_map.108), channel_id=1, replica_groups=mesh['gx'=32,'gy'=8,'gz'=2] {'gy','gz'}, dimensions={0} | all-to-all | bytes 131072 | tf_op jit(solution)/shard_map/all_to_all | solution.py:699
  108.0 1.7 %shard_map.109 = (f32[8,4,8]{2,1,0:T(4,128)}, f32[256,3]{1,0:T(8,128)}) custom-call(s32[2]{0:T(128)} %pad_add_fusion.place_ref, f32[16,8,128]{2,1,0:T(8,128)} %all_to_all.5.got_ref), custom_call_target="tpu_custom_call" | custom-call | flops 1000000 | bytes 100000 | tf_op jit(solution)/shard_map/pallas_call | solution.py:700
  109.7 1.8 %copy.12 = f32[2,4,4,8,3]{3,2,4,1,0:T(4,128)} copy(f32[2,4,4,8,3]{4,3,2,1,0:T(8,128)} %bitcast.14) | data formatting | bytes 6144
  (11 shorter events, 0.0 us)
Async XLA Ops:
  4.3 19.5 %collective-permute-start = (f32[40,128]{1,0:T(8,128)}, f32[40,128]{1,0:T(8,128)S(1)}, u32[]{:S(2)}, u32[]{:S(2)}) collective-permute-start(f32[40,128]{1,0:T(8,128)} %get-tuple-element.21), channel_id=1, source_target_pairs={{0,2},{1,15},{2,4},{3,1},{4,6},{5,3},{6,8},{7,5},{8,10},{9,7},{10,... | collective-permute-start | bytes 61448 | tf_op jit(solution)/shard_map/ppermute | solution.py:638
  8.9 15.0 %collective-permute-start.1 = (f32[40,128]{1,0:T(8,128)}, f32[40,128]{1,0:T(8,128)S(1)}, u32[]{:S(2)}, u32[]{:S(2)}) collective-permute-start(f32[40,128]{1,0:T(8,128)} %get-tuple-element.22), channel_id=1, source_target_pairs={{0,15},{1,2},{2,1},{3,4},{4,3},{5,6},{6,5},{7,8},{8,7},{9,10},{10,... | collective-permute-start | bytes 61448 | tf_op jit(solution)/shard_map/ppermute | solution.py:639
  23.9 0.6 copy-start
  23.9 0.6 copy-start.1
  26.2 16.6 %collective-permute-start.3 = (f32[88,128]{1,0:T(8,128)}, f32[88,128]{1,0:T(8,128)S(1)}, u32[]{:S(2)}, u32[]{:S(2)}) collective-permute-start(f32[88,128]{1,0:T(8,128)} %get-tuple-element.23.lown_ref), channel_id=1, source_target_pairs={{16,0},{32,16},{48,32},{64,48},{80,64},{96,80},{112,96},{128,112},... | collective-permute-start | bytes 135176 | tf_op jit(solution)/shard_map/ppermute | solution.py:648
  38.4 8.8 %collective-permute-start.2 = (f32[88,128]{1,0:T(8,128)}, f32[88,128]{1,0:T(8,128)S(1)}, u32[]{:S(2)}, u32[]{:S(2)}) collective-permute-start(f32[88,128]{1,0:T(8,128)} %get-tuple-element.24.rown_ref), channel_id=1, source_target_pairs={{0,16},{16,32},{32,48},{48,64},{64,80},{80,96},{96,112},{112,128},... | collective-permute-start | bytes 135176 | tf_op jit(solution)/shard_map/ppermute | solution.py:647
  42.9 4.3 %copy-start.4 = (f32[88,128]{1,0:T(8,128)}, f32[88,128]{1,0:T(8,128)S(1)}, u32[]{:S(2)}) copy-start(f32[88,128]{1,0:T(8,128)S(1)} %collective-permute-done.3.fromr_ref) | copy-start | bytes 135172
  47.1 0.6 copy-start.5
  81.4 9.3 %collective-permute-start.4 = (f32[24,128]{1,0:T(8,128)}, f32[24,128]{1,0:T(8,128)S(1)}, u32[]{:S(2)}, u32[]{:S(2)}) collective-permute-start(f32[24,128]{1,0:T(8,128)} %get-tuple-element.34), channel_id=1, source_target_pairs={{0,16},{16,32},{32,48},{48,64},{64,80},{80,96},{96,112},{112,128},... | collective-permute-start | bytes 36872 | tf_op jit(solution)/shard_map/ppermute | solution.py:697
  83.3 7.7 %collective-permute-start.5 = (f32[24,128]{1,0:T(8,128)}, f32[24,128]{1,0:T(8,128)S(1)}, u32[]{:S(2)}, u32[]{:S(2)}) collective-permute-start(f32[24,128]{1,0:T(8,128)} %get-tuple-element.35), channel_id=1, source_target_pairs={{16,0},{32,16},{48,32},{64,48},{80,64},{96,80},{112,96},{128,112},... | collective-permute-start | bytes 36872 | tf_op jit(solution)/shard_map/ppermute | solution.py:696
  90.7 0.6 copy-start.2
  91.1 0.6 copy-start.3

commit v2 on v1

--- a/solution.py
+++ b/solution.py
@@ -55,21 +55,39 @@
     return iota(shape, len(shape) - 1)
 
 
-def pack_kernel(gz_ref, pos_ref, spec_ref, nbr_ref, mask_ref, own_ref, straight_ref, cross_ref):
+def block_masks(count):
+    row, lane = iota((32 * count, 256), 0), iota((32 * count, 256), 1)
+    keep = (lane // 32 == row // (4 * count)) & ((lane // 8) % 4 == row % 4)
+    spread8 = jnp.where(iota((8, 256), 1) % 8 == iota((8, 256), 0), 1.0, 0.0).astype(bf16)
+    return keep, spread8
+
+
+def pack_kernel(
+    gz_ref, pos_hbm, spec_hbm, nbr_hbm, mask_hbm, own_ref, straight_ref, cross_ref, pos_ref, spec_ref, nbr_ref, mask_ref, sems
+):
+    copies = [
+        pltpu.make_async_copy(src, dst, sems.at[i])
+        for i, (src, dst) in enumerate(
+            ((nbr_hbm, nbr_ref), (mask_hbm, mask_ref), (pos_hbm, pos_ref), (spec_hbm, spec_ref))
+        )
+    ]
+    for copy in copies:
+        copy.start()
+    for copy in copies:
+        copy.wait()
     eye16 = jnp.where(iota((E, E), 0) == iota((E, E), 1), 1.0, 0.0).astype(bf16)
     own_ref[0:16, :] = dot(eye16, nbr_ref[...].astype(f32).astype(bf16), ((1,), (1,)))
     own_ref[16:32, :] = dot(eye16, mask_ref[...].astype(f32).astype(bf16), ((1,), (1,)))
-    eye3 = jnp.where(iota((8, 3), 0) == iota((8, 3), 1), 1.0, 0.0).astype(bf16)
-    high, mid, low = split3(pos_ref[...])
-    nt = ((1,), (1,))
-    tail = (dot(eye3, high, nt) + dot(eye3, mid, nt)) + dot(eye3, low, nt)
-    lane, slot = iota((8, 256), 1), iota((8, 256), 0)
-    total = jnp.zeros((4, 256), f32)
-    for i in range(8):
-        pick = jnp.where((lane % 8 == slot) & (lane // 32 == i), 1.0, 0.0).astype(bf16)
-        total = total + dot(spec_ref[i].astype(f32).astype(bf16), pick)
-    keep = (iota((4, 256), 1) // 8) % 4 == iota((4, 256), 0)
-    species = jnp.sum(jnp.where(keep, total, 0.0), 0, keepdims=True)
+    keep, spread8 = block_masks(3)
+    group = jnp.where((iota((8, 96), 1) // 4) % 3 == iota((8, 96), 0), 1.0, 0.0).astype(bf16)
+    tail = None
+    for part in split3(pos_ref[...]):
+        rows = jnp.where(keep, dot(part, spread8), 0.0).astype(bf16)
+        piece = dot(group, rows)
+        tail = piece if tail is None else tail + piece
+    keep, _ = block_masks(1)
+    kinds = jnp.where(keep, dot(spec_ref[...].astype(f32).astype(bf16), spread8), 0.0)
+    species = jnp.sum(kinds, 0, keepdims=True)
     own_ref[32:40, :] = jnp.where(iota((8, 256), 0) == 3, species, tail)
 
     lower = lanes((40, L)) < 64
@@ -117,7 +135,9 @@
             out[24 + 32 * r : 56 + 32 * r, :] = halves(tiles[r][0:32], tiles[r + 1][0:32])
 
 
-def weights_kernel(emb_ref, rad_ref, mix_ref, read_ref, vf_ref, vb_ref, wf_ref, wb_ref, mf_ref, mb_ref, et_ref, ro_ref):
+def weights_kernel(
+    emb_ref, rad_ref, mix_ref, read_ref, off_ref, vf_ref, vb_ref, wf_ref, wb_ref, mf_ref, mb_ref, et_ref, ro_ref, eo_ref
+):
     emb = emb_ref[...]
     for q in range(3):
         base = rad_ref[0, :, q * C : (q + 1) * C] * SCALE
@@ -154,6 +174,8 @@
     stack = jnp.concatenate([high.astype(f32), mid.astype(f32), low.astype(f32), jnp.zeros((4, C), f32)], 0)
     et_ref[...] = stack.T.astype(bf16)
     ro_ref[...] = jnp.broadcast_to(read_ref[...], (C, L)).T
+    pick = jnp.where(iota((4, 4), 0) == iota((4, 4), 1), off_ref[...], 0.0)
+    eo_ref[...] = jnp.broadcast_to(jnp.sum(pick, 1, keepdims=True), (4, L))
 
 
 def decode(ids):
@@ -191,8 +213,8 @@
 
 
 def main_kernel(
-    off_ref, lown_ref, rown_ref, froml_ref, fromr_ref,
-    vf_ref, vb_ref, wf_ref, wb_ref, mf_ref, mb_ref, et_ref, ro_ref,
+    lown_ref, rown_ref, froml_ref, fromr_ref,
+    vf_ref, vb_ref, wf_ref, wb_ref, mf_ref, mb_ref, et_ref, ro_ref, eo_ref,
     outl_ref, outo_ref, outr_ref,
     table, edges, geo, basis, slope, moment, hid, dsilu, dhid, dmom, inv, geo2, rb2, rbst, hg, onehot,
     hs, rad2, efac, dhs, drad, extra, pick, force,
@@ -382,7 +404,7 @@
         kind = table[(x + 2) * 3 + 1, 3:4, :]
         offset = jnp.zeros((1, L), f32)
         for k in range(4):
-            offset = jnp.where(kind == float(k), off_ref[k], offset)
+            offset = jnp.where(kind == float(k), eo_ref[k : k + 1, :], offset)
         energy = jnp.sum(read * h2, 0, keepdims=True) + offset
         geo2[RAD, 0:1, :] = energy
         extra[x, 0, 0, 0:1, :] = energy
@@ -538,8 +560,8 @@
                 out[at + 3 : at + 4, :] = extra[plane - 2, 0, 0, 0:1, :]
 
 
-def chunk_kernel(place_ref, own_ref, left_ref, right_ref, out_ref):
-    gy, gz = place_ref[0], place_ref[1]
+def chunk_kernel(gy_ref, gz_ref, own_ref, left_ref, right_ref, out_ref):
+    gy, gz = gy_ref[0], gz_ref[0]
     front = gz == 0
     total = own_ref[...] + left_ref[...] + right_ref[...]
     quarter = lanes((4, L)) // 32
@@ -565,8 +587,8 @@
         out_ref[beside * 2 + zh, 0:4, :] = near
 
 
-def unpack_kernel(place_ref, got_ref, energy_ref, force_ref):
-    gy = place_ref[0]
+def unpack_kernel(gy_ref, got_ref, energy_ref, force_ref):
+    gy = gy_ref[0]
     y_count = got_ref.shape[0] // 2
     below = jnp.where(gy == 0, y_count - 1, gy - 1)
     above = jnp.where(gy == y_count - 1, 0, gy + 1)
@@ -577,29 +599,33 @@
     first = jnp.where(lower, low, roll(high, 64))
     second = jnp.where(lower, roll(low, 64), high)
     rows = jnp.concatenate([first, second], 1)
+    keep, spread8 = block_masks(3)
+    group = jnp.where((iota((96, 8), 0) // 4) % 3 == iota((96, 8), 1), 1.0, 0.0).astype(bf16)
     rows8 = jnp.concatenate([rows, jnp.zeros((4, 256), f32)], 0)
-    force_ref[...] = rows8.T[:, 0:3]
-    pick = jnp.where(iota((8, 256), 1) % 8 == iota((8, 256), 0), 1.0, 0.0).astype(bf16)
-    high, mid, low = split3(rows[3:4])
-    lane, cell = iota((4, 256), 1), iota((4, 256), 0)
     nt = ((1,), (1,))
-    for i in range(8):
-        keep = lane // 8 == cell + 4 * i
-        total = None
-        for part in (high, mid, low):
-            piece = dot(jnp.where(keep, part.astype(f32), 0.0).astype(bf16), pick, nt)
-            total = piece if total is None else total + piece
-        energy_ref[i] = total
-
-
-def call(kernel, outs, in_specs, scratch=(), flops=10**6):
+    total = None
+    for part in split3(rows8):
+        wide = jnp.where(keep, dot(group, part), 0.0).astype(bf16)
+        piece = dot(wide, spread8, nt)
+        total = piece if total is None else total + piece
+    force_ref[...] = total
+    keep, _ = block_masks(1)
+    total = None
+    for part in split3(rows[3:4]):
+        wide = jnp.where(keep, part.astype(f32), 0.0).astype(bf16)
+        piece = dot(wide, spread8, nt)
+        total = piece if total is None else total + piece
+    energy_ref[...] = total
+
+
+def call(kernel, outs, in_specs, scratch=(), flops=10**6, vmem=4):
     return pl.pallas_call(
         kernel,
         out_shape=outs,
         in_specs=in_specs,
         out_specs=jax.tree.map(lambda _: pl.BlockSpec(memory_space=VMEM), outs),
         scratch_shapes=list(scratch),
-        compiler_params=pltpu.CompilerParams(vmem_limit_bytes=60 * 2**20),
+        compiler_params=pltpu.CompilerParams(vmem_limit_bytes=int(vmem * 2**20)),
         cost_estimate=pl.CostEstimate(flops=flops, bytes_accessed=10**5, transcendentals=0),
     )
 
@@ -616,15 +642,19 @@
     gy_count, gz_count = lax.axis_size("gy"), lax.axis_size("gz")
     gx_count = lax.axis_size("gx")
     gy, gz = lax.axis_index("gy"), lax.axis_index("gz")
-    place = jnp.stack([gy, gz]).astype(i32)
+    gy_only = gy.astype(i32).reshape(1)
     gz_only = gz.astype(i32).reshape(1)
 
     own, straight, cross = call(
-        pack_kernel, [shape(40, 256), shape(40, L), shape(40, L)], [sm, v, v, v, v]
+        pack_kernel,
+        [shape(40, 256), shape(40, L), shape(40, L)],
+        [sm] + [pl.BlockSpec(memory_space=pltpu.HBM)] * 4,
+        [VMEM((96, 8), f32), VMEM((32, 8), i32), VMEM((256, E), i32), VMEM((256, E), i32), pltpu.SemaphoreType.DMA((4,))],
+        vmem=53.8,
     )(
         gz_only,
-        positions.reshape(256, 3),
-        species.reshape(8, 4, 8),
+        positions.transpose(0, 1, 4, 2, 3).reshape(96, 8),
+        species.reshape(32, 8),
         neighbors.reshape(256, E),
         edge_mask.reshape(256, E),
     )
@@ -658,10 +688,12 @@
             shape(2, 384, 384, dtype=bf16),
             shape(C, 16, dtype=bf16),
             shape(C, L),
+            shape(4, L),
         ],
-        [v, v, v, v],
+        [v] * 5,
         flops=10**7,
-    )(species_embed, radial_weight, mix_weight, readout.reshape(1, C))
+        vmem=8,
+    )(species_embed, radial_weight, mix_weight, readout.reshape(1, C), energy_offset.reshape(1, 4))
 
     scratch = [
         VMEM((18, 8, L), f32),
@@ -690,15 +722,15 @@
         VMEM((18, 8, L), f32),
     ]
     out_left, out_own, out_right = call(
-        main_kernel, [shape(24, L)] * 3, [sm] + [v] * 12, scratch, flops=10**9
-    )(energy_offset, left, right, from_left, from_right, *weights)
+        main_kernel, [shape(24, L)] * 3, [v] * 13, scratch, flops=10**9, vmem=48
+    )(left, right, from_left, from_right, *weights)
 
     back_right = lax.ppermute(out_left, "gx", down)
     back_left = lax.ppermute(out_right, "gx", up)
-    chunks = call(chunk_kernel, shape(gy_count * 2, 8, L), [sm, v, v, v])(place, out_own, back_left, back_right)
+    chunks = call(chunk_kernel, shape(gy_count * 2, 8, L), [sm, sm, v, v, v])(gy_only, gz_only, out_own, back_left, back_right)
     got = lax.all_to_all(chunks, yz, 0, 0)
-    energy, force = call(unpack_kernel, [shape(8, 4, 8), shape(256, 3)], [sm, v])(place, got)
-    return energy.reshape(2, 4, 4, 8), force.reshape(2, 4, 4, 8, 3)
+    energy, force = call(unpack_kernel, [shape(32, 8), shape(96, 8)], [sm, v])(gy_only, got)
+    return energy.reshape(2, 4, 4, 8), force.reshape(2, 4, 3, 4, 8).transpose(0, 1, 3, 4, 2)
 
 
 def solution(mesh):

time: 112 us -> 101 us (0.902)
  Pallas kernels: 43.2 us -> 34.9 us
  local copies, waits for them, and re-layouts: 5.3 us -> 1.4 us
  waiting for transfers between devices: 4.63 us -> 5.82 us
    pallas_call x4, Pallas kernels: 38.9 us -> 34.2 us  [the longest x1 31.7 us: shards(): call(main_kernel, [shape(24, L)] * 3, [v] * 13, scratch, flops=10 ** 9, v...]
    unnamed x14 -> x12, local copies, waits for them, and re-layouts: 5.3 us -> 1.4 us
    pallas_call x1, Pallas kernels: 2.56 us -> 0.48 us  [shards(): call(weights_kernel, [shape(3, C, 96, dtype=bf16), shape(3, 64, 256, dtyp...]
    all_gather x1, blocking collectives: 8.45 us -> 10.4 us  [shards(): both = lax.all_gather(own, 'gz')]
    all_to_all x1, blocking collectives: 14.8 us -> 13.3 us  [shards(): got = lax.all_to_all(chunks, yz, 0, 0)]
    pallas_call x1, Pallas kernels: 1.74 us -> 0.23 us  [shards(): call(rows_kernel, [shape(88, L), shape(88, L)], [sm, v, v, v])]
  transfers between devices with their start and end apart: 6 -> 6, of which waited for: 2 -> 2; matrix products, arithmetic and copies ran while one was open for 1% -> 0% of each run, Pallas kernels for 2% -> 0%
where the time goes in v2:
time: 101 us; the launch traced here: 100 us
  Pallas kernels  34.9 us (35%)
  starting transfers between devices  33.7 us (33%)
  blocking collectives  23.7 us (23%)
  waiting for transfers between devices  5.82 us (6%)
  local copies, waits for them, and re-layouts  1.4 us (1%)
    pallas_call x1, Pallas kernels, shards(): call(main_kernel, [shape(24, L)] * 3, [v] * 13, scratch, flops=10 ** 9, v...  31.7 us
    all_to_all x1, blocking collectives, shards(): got = lax.all_to_all(chunks, yz, 0, 0)  13.3 us
    ppermute x1, starting transfers between devices, shards(): from_right = lax.ppermute(left, 'gx', down)  12.1 us
    all_gather x1, blocking collectives, shards(): both = lax.all_gather(own, 'gz')  10.4 us
    ppermute x1, starting transfers between devices, shards(): back_right = lax.ppermute(out_left, 'gx', down)  6.68 us
    ppermute x1, starting transfers between devices, shards(): near_cross = lax.ppermute(cross, yz, go_cross)  6.5 us
    ppermute x1, waiting for transfers between devices, shards(): from_left = lax.ppermute(right, 'gx', up)  5.02 us
    ppermute x1, starting transfers between devices, shards(): near_straight = lax.ppermute(straight, yz, go_straight)  4.59 us
  transfers between devices with their start and end apart: 6, of which 2 were waited for; matrix products, arithmetic and copies ran while one was open for 0% of the time, Pallas kernels for 0%

profile of v2, /device:TPU:1, one launch (start us, length us, event | category | flops | bytes accessed | tf_op | source)
XLA Modules:
  0.0 100.4 jit_solution(5583144576621117205)
XLA Ops:
  0.7 0.8 copy-done.2
  1.4 1.4 %shard_map.104 = (f32[40,256]{1,0:T(8,128)S(1)}, f32[40,128]{1,0:T(8,128)S(1)}, f32[40,128]{1,0:T(8,128)S(1)}) custom-call(s32[1]{0:T(128)} %bitcast.1.gz_ref, f32[96,8]{1,0:T(8,128)} %bitcast.21, s32[32,8]{1,0:T(8,128)S(1)} %bitcast.16, s32[256,16]{1,0:T(8,128)} %bitcast.19, s32[256,16]{1,0:T(8,128)} %bitcast.20), custom_call_target="tpu_custom_call" | custom-call | flops 1000000 | bytes 100000 | tf_op jit(solution)/shard_map/pallas_call | solution.py:648
  2.8 4.6 %collective-permute-start = (f32[40,128]{1,0:T(8,128)S(1)}, f32[40,128]{1,0:T(8,128)S(1)}, u32[]{:S(2)}, u32[]{:S(2)}) collective-permute-start(f32[40,128]{1,0:T(8,128)S(1)} %get-tuple-element.22), channel_id=1, source_target_pairs={{0,2},{1,15},{2,4},{3,1},{4,6},{5,3},{6,8},{7,5},{8,10},{9,7},{10,... | collective-permute-start | bytes 61448 | tf_op jit(solution)/shard_map/ppermute | solution.py:668
  7.4 6.5 %collective-permute-start.1 = (f32[40,128]{1,0:T(8,128)S(1)}, f32[40,128]{1,0:T(8,128)S(1)}, u32[]{:S(2)}, u32[]{:S(2)}) collective-permute-start(f32[40,128]{1,0:T(8,128)S(1)} %get-tuple-element.23), channel_id=1, source_target_pairs={{0,15},{1,2},{2,1},{3,4},{4,3},{5,6},{6,5},{7,8},{8,7},{9,10},{10,... | collective-permute-start | bytes 61448 | tf_op jit(solution)/shard_map/ppermute | solution.py:669
  13.9 10.4 %all-gather = f32[80,256]{1,0:T(8,128)S(1)} all-gather(f32[40,256]{1,0:T(8,128)S(1)} %get-tuple-element.21), channel_id=2, replica_groups=mesh['gx'=32,'gy'=8,'gz'=2] {'gz'}, dimensions={0}, use_global_device_ids=true | all-gather | bytes 122880 | tf_op jit(solution)/shard_map/all_gather | solution.py:670
  24.4 0.0 collective-permute-done.straight_ref
  24.4 0.2 shard_map.105
  24.6 12.1 %collective-permute-start.3 = (f32[88,128]{1,0:T(8,128)S(1)}, f32[88,128]{1,0:T(8,128)S(1)}, u32[]{:S(2)}, u32[]{:S(2)}) collective-permute-start(f32[88,128]{1,0:T(8,128)S(1)} %get-tuple-element.24.lown_ref), channel_id=1, source_target_pairs={{16,0},{32,16},{48,32},{64,48},{80,64},{96,80},{112,96},{128,112},... | collective-permute-start | bytes 135176 | tf_op jit(solution)/shard_map/ppermute | solution.py:678
  36.8 0.0 copy-start.3
  36.8 1.9 %collective-permute-start.2 = (f32[88,128]{1,0:T(8,128)S(1)}, f32[88,128]{1,0:T(8,128)S(1)}, u32[]{:S(2)}, u32[]{:S(2)}) collective-permute-start(f32[88,128]{1,0:T(8,128)S(1)} %get-tuple-element.25.rown_ref), channel_id=1, source_target_pairs={{0,16},{16,32},{32,48},{48,64},{64,80},{80,96},{96,112},{112,128},... | collective-permute-start | bytes 135176 | tf_op jit(solution)/shard_map/ppermute | solution.py:677
  38.7 0.0 copy-start.4
  38.7 0.0 copy-start.5
  38.7 0.6 copy-done.4
  39.4 0.0 copy-done.5
  39.4 0.5 shard_map.106
  39.9 5.0 %collective-permute-done.2.froml_ref = f32[88,128]{1,0:T(8,128)S(1)} collective-permute-done((f32[88,128]{1,0:T(8,128)S(1)}, f32[88,128]{1,0:T(8,128)S(1)}, u32[]{:S(2)}, u32[]{:S(2)}) %collective-permute-start.2) | collective-permute-done | bytes 45088 | tf_op jit(solution)/shard_map/ppermute | solution.py:677
  44.9 31.7 %shard_map.107 = (f32[24,128]{1,0:T(8,128)S(1)}, f32[24,128]{1,0:T(8,128)S(1)}, f32[24,128]{1,0:T(8,128)S(1)}) custom-call(f32[88,128]{1,0:T(8,128)S(1)} %get-tuple-element.24.lown_ref, f32[88,128]{1,0:T(8,128)S(1)} %get-tuple-element.25.rown_ref, f32[88,128]{1,0:T(8,128)S(1)} %collective-permute-done.2.froml_ref, ...), custom_call_target="tpu_custom_call" | custom-call | flops 1000000000 | bytes 100000 | tf_op jit(solution)/shard_map/pallas_call | solution.py:724
  76.5 1.9 %collective-permute-start.4 = (f32[24,128]{1,0:T(8,128)S(1)}, f32[24,128]{1,0:T(8,128)S(1)}, u32[]{:S(2)}, u32[]{:S(2)}) collective-permute-start(f32[24,128]{1,0:T(8,128)S(1)} %get-tuple-element.36), channel_id=1, source_target_pairs={{0,16},{16,32},{32,48},{48,64},{64,80},{80,96},{96,112},{112,128},... | collective-permute-start | bytes 36872 | tf_op jit(solution)/shard_map/ppermute | solution.py:729
  78.5 6.7 %collective-permute-start.5 = (f32[24,128]{1,0:T(8,128)S(1)}, f32[24,128]{1,0:T(8,128)S(1)}, u32[]{:S(2)}, u32[]{:S(2)}) collective-permute-start(f32[24,128]{1,0:T(8,128)S(1)} %get-tuple-element.37), channel_id=1, source_target_pairs={{16,0},{32,16},{48,32},{64,48},{80,64},{96,80},{112,96},{128,112},... | collective-permute-start | bytes 36872 | tf_op jit(solution)/shard_map/ppermute | solution.py:728
  85.2 0.0 collective-permute-done.4.left_ref
  85.2 0.8 collective-permute-done.5.right_ref
  86.0 0.1 shard_map.108
  86.1 13.3 %all_to_all.5.got_ref = f32[16,8,128]{2,1,0:T(8,128)S(1)} all-to-all(f32[16,8,128]{2,1,0:T(8,128)S(1)} %shard_map.108), channel_id=1, replica_groups=mesh['gx'=32,'gy'=8,'gz'=2] {'gy','gz'}, dimensions={0} | all-to-all | bytes 131072 | tf_op jit(solution)/shard_map/all_to_all | solution.py:731
  99.4 1.0 %shard_map.109 = (f32[32,8]{1,0:T(8,128)}, f32[96,8]{1,0:T(8,128)}) custom-call(s32[1]{0:T(128)} %bitcast.gy_ref, f32[16,8,128]{2,1,0:T(8,128)S(1)} %all_to_all.5.got_ref), custom_call_target="tpu_custom_call" | custom-call | flops 1000000 | bytes 100000 | tf_op jit(solution)/shard_map/pallas_call | solution.py:732
  (8 shorter events, 0.0 us)
Async XLA Ops:
  0.6 38.1 %copy-start = (f32[2,384,128]{2,1,0:T(8,128)S(1)}, f32[2,384,128]{2,1,0:T(8,128)}, u32[]{:S(2)}) copy-start(f32[2,384,128]{2,1,0:T(8,128)} %mix_ref.1) | copy-start | bytes 1179652
  0.6 0.8 copy-start.2
  2.8 21.6 %collective-permute-start = (f32[40,128]{1,0:T(8,128)S(1)}, f32[40,128]{1,0:T(8,128)S(1)}, u32[]{:S(2)}, u32[]{:S(2)}) collective-permute-start(f32[40,128]{1,0:T(8,128)S(1)} %get-tuple-element.22), channel_id=1, source_target_pairs={{0,2},{1,15},{2,4},{3,1},{4,6},{5,3},{6,8},{7,5},{8,10},{9,7},{10,... | collective-permute-start | bytes 61448 | tf_op jit(solution)/shard_map/ppermute | solution.py:668
  7.4 17.0 %collective-permute-start.1 = (f32[40,128]{1,0:T(8,128)S(1)}, f32[40,128]{1,0:T(8,128)S(1)}, u32[]{:S(2)}, u32[]{:S(2)}) collective-permute-start(f32[40,128]{1,0:T(8,128)S(1)} %get-tuple-element.23), channel_id=1, source_target_pairs={{0,15},{1,2},{2,1},{3,4},{4,3},{5,6},{6,5},{7,8},{8,7},{9,10},{10,... | collective-permute-start | bytes 61448 | tf_op jit(solution)/shard_map/ppermute | solution.py:669
  24.4 14.3 %copy-start.1 = (f32[2,8,384]{2,1,0:T(8,128)S(1)}, f32[2,8,384]{2,1,0:T(8,128)}, u32[]{:S(2)}) copy-start(f32[2,8,384]{2,1,0:T(8,128)} %rad_ref.1) | copy-start | bytes 73732
  24.6 15.2 %collective-permute-start.3 = (f32[88,128]{1,0:T(8,128)S(1)}, f32[88,128]{1,0:T(8,128)S(1)}, u32[]{:S(2)}, u32[]{:S(2)}) collective-permute-start(f32[88,128]{1,0:T(8,128)S(1)} %get-tuple-element.24.lown_ref), channel_id=1, source_target_pairs={{16,0},{32,16},{48,32},{64,48},{80,64},{96,80},{112,96},{128,112},... | collective-permute-start | bytes 135176 | tf_op jit(solution)/shard_map/ppermute | solution.py:678
  36.8 2.0 %copy-start.3 = (f32[4,128]{1,0:T(4,128)S(1)}, f32[4,128]{1,0:T(4,128)}, u32[]{:S(2)}) copy-start(f32[4,128]{1,0:T(4,128)} %emb_ref.1) | copy-start | bytes 6148
  36.8 8.1 %collective-permute-start.2 = (f32[88,128]{1,0:T(8,128)S(1)}, f32[88,128]{1,0:T(8,128)S(1)}, u32[]{:S(2)}, u32[]{:S(2)}) collective-permute-start(f32[88,128]{1,0:T(8,128)S(1)} %get-tuple-element.25.rown_ref), channel_id=1, source_target_pairs={{0,16},{16,32},{32,48},{48,64},{64,80},{80,96},{96,112},{112,128},... | collective-permute-start | bytes 135176 | tf_op jit(solution)/shard_map/ppermute | solution.py:677
  38.7 0.7 copy-start.4
  38.7 0.7 copy-start.5
  76.5 8.6 %collective-permute-start.4 = (f32[24,128]{1,0:T(8,128)S(1)}, f32[24,128]{1,0:T(8,128)S(1)}, u32[]{:S(2)}, u32[]{:S(2)}) collective-permute-start(f32[24,128]{1,0:T(8,128)S(1)} %get-tuple-element.36), channel_id=1, source_target_pairs={{0,16},{16,32},{32,48},{48,64},{64,80},{80,96},{96,112},{112,128},... | collective-permute-start | bytes 36872 | tf_op jit(solution)/shard_map/ppermute | solution.py:729
  78.5 7.5 %collective-permute-start.5 = (f32[24,128]{1,0:T(8,128)S(1)}, f32[24,128]{1,0:T(8,128)S(1)}, u32[]{:S(2)}, u32[]{:S(2)}) collective-permute-start(f32[24,128]{1,0:T(8,128)S(1)} %get-tuple-element.37), channel_id=1, source_target_pairs={{16,0},{32,16},{48,32},{64,48},{80,64},{96,80},{112,96},{128,112},... | collective-permute-start | bytes 36872 | tf_op jit(solution)/shard_map/ppermute | solution.py:728

commit v3 on v2

v3 whole, which is shorter than its diff:
```python
import math

import jax
import jax.numpy as jnp
from jax import lax
from jax.experimental import pallas as pl
from jax.experimental.pallas import tpu as pltpu
from jax.sharding import PartitionSpec as P

f32 = jnp.float32
bf16 = jnp.bfloat16
i32 = jnp.int32

E = 16
C = 128
NB = 8
L = 128
CUT = 2.0
GAMMA = ((NB - 1) / CUT) ** 2
SCALE = E**-0.5
R3 = math.sqrt(3.0)
R5 = math.sqrt(5.0)
R15 = math.sqrt(15.0)
VMEM = pltpu.VMEM
SMEM = pltpu.SMEM


def split2(x):
    return x, x - x.astype(bf16).astype(f32)


def split3(x):
    high = x.astype(bf16)
    rest = x - high.astype(f32)
    mid = rest.astype(bf16)
    low = (rest - mid.astype(f32)).astype(bf16)
    return high, mid, low


def dot(a, b, dims=((1,), (0,))):
    return lax.dot_general(a, b, (dims, ((), ())), preferred_element_type=f32)


def iota(shape, dim):
    return lax.broadcasted_iota(i32, shape, dim)


def roll(x, shift):
    return pltpu.roll(x, shift % x.shape[-1], x.ndim - 1)


def lanes(shape):
    return iota(shape, len(shape) - 1)


def block_masks(count):
    row, lane = iota((32 * count, 256), 0), iota((32 * count, 256), 1)
    keep = (lane // 32 == row // (4 * count)) & ((lane // 8) % 4 == row % 4)
    spread8 = jnp.where(iota((8, 256), 1) % 8 == iota((8, 256), 0), 1.0, 0.0).astype(bf16)
    return keep, spread8


def pack_kernel(
    gz_ref, pos_hbm, spec_hbm, nbr_hbm, mask_hbm, own_ref, straight_ref, cross_ref, pos_ref, spec_ref, nbr_ref, mask_ref, sems
):
    copies = [
        pltpu.make_async_copy(src, dst, sems.at[i])
        for i, (src, dst) in enumerate(
            ((nbr_hbm, nbr_ref), (mask_hbm, mask_ref), (pos_hbm, pos_ref), (spec_hbm, spec_ref))
        )
    ]
    for copy in copies:
        copy.start()
    for copy in copies:
        copy.wait()
    eye16 = jnp.where(iota((E, E), 0) == iota((E, E), 1), 1.0, 0.0).astype(bf16)
    own_ref[0:16, :] = dot(eye16, nbr_ref[...].astype(f32).astype(bf16), ((1,), (1,)))
    own_ref[16:32, :] = dot(eye16, mask_ref[...].astype(f32).astype(bf16), ((1,), (1,)))
    keep, spread8 = block_masks(3)
    group = jnp.where((iota((8, 96), 1) // 4) % 3 == iota((8, 96), 0), 1.0, 0.0).astype(bf16)
    tail = None
    for part in split3(pos_ref[...]):
        rows = jnp.where(keep, dot(part, spread8), 0.0).astype(bf16)
        piece = dot(group, rows)
        tail = piece if tail is None else tail + piece
    keep, _ = block_masks(1)
    kinds = jnp.where(keep, dot(spec_ref[...].astype(f32).astype(bf16), spread8), 0.0)
    species = jnp.sum(kinds, 0, keepdims=True)
    own_ref[32:40, :] = jnp.where(iota((8, 256), 0) == 3, species, tail)

    lower = lanes((40, L)) < 64
    first, second = own_ref[:, 0:128], own_ref[:, 128:256]
    rows_low = jnp.where(lower, first, roll(second, 64))
    rows_high = jnp.where(lower, roll(first, 64), second)
    front = gz_ref[0] == 0
    straight_ref[...] = jnp.where(front, rows_high, rows_low)
    cross_ref[...] = jnp.where(front, rows_low, rows_high)


def spread(half0, half1, start):
    quarter = lanes((40, L)) // 32
    out = roll(half0, -start)
    out = jnp.where(quarter == 1, roll(half1, 32 - start), out)
    out = jnp.where(quarter == 2, roll(half0, 32 - start), out)
    return jnp.where(quarter == 3, roll(half1, 64 - start), out)


def halves(first, second):
    return roll(jnp.where(lanes(first.shape) >= 64, first, second), 64)


def rows_kernel(gz_ref, all_ref, straight_ref, cross_ref, left_ref, right_ref):
    front = gz_ref[0] == 0
    near0 = jnp.where(front, straight_ref[...], cross_ref[...])
    near1 = jnp.where(front, cross_ref[...], straight_ref[...])
    for x in range(2):
        near = spread(near0, near1, 64 * x)
        own = [
            spread(all_ref[0, :, x * L : (x + 1) * L], all_ref[1, :, x * L : (x + 1) * L], 64 * pair)
            for pair in range(2)
        ]
        tiles = [
            jnp.where(front, near, own[0]),
            jnp.where(front, own[0], own[1]),
            jnp.where(front, own[1], near),
        ]
        for pair in range(3):
            at = (x * 3 + pair) * 4
            left_ref[at : at + 4, :] = tiles[pair][32:36]
            right_ref[at : at + 4, :] = tiles[pair][32:36]
        out = left_ref if x == 0 else right_ref
        for r in range(2):
            out[24 + 32 * r : 56 + 32 * r, :] = halves(tiles[r][0:32], tiles[r + 1][0:32])


def weights_kernel(
    emb_ref, rad_ref, mix_ref, read_ref, off_ref, vf_ref, vb_ref, wf_ref, wb_ref, mf_ref, mb_ref, et_ref, ro_ref, eo_ref
):
    emb = emb_ref[...]
    for q in range(3):
        base = rad_ref[0, :, q * C : (q + 1) * C] * SCALE
        v = jnp.concatenate([base * emb[k : k + 1] for k in range(4)], 0)
        high, low = split2(v)
        vb_ref[q, 0:32, 0:128] = high
        vb_ref[q, 0:32, 128:256] = high
        vb_ref[q, 32:64, 0:128] = low
        vb_ref[q, 32:64, 128:256] = jnp.zeros((32, 128), f32)
        high, low = split2(v.T)
        vf_ref[q] = jnp.concatenate([high, high, low], 1)
        w = rad_ref[1, :, q * C : (q + 1) * C]
        both = jnp.concatenate(split2(w), 0)
        wb_ref[q, :, 0:128] = both
        wb_ref[q, :, 128:256] = jnp.where(iota((16, 128), 0) < 8, both, 0.0)
        high, low = split2(w.T)
        wf_ref[q] = jnp.concatenate([high, high, low], 1)
    for layer in range(2):
        for q in range(3):
            m = mix_ref[layer, q * C : (q + 1) * C, :]
            high, low = split2(m)
            mb_ref[layer, q * C : (q + 1) * C, 0:128] = high
            mb_ref[layer, q * C : (q + 1) * C, 128:256] = high
            mb_ref[layer, q * C : (q + 1) * C, 256:384] = low
            high, low = split2(m.T)
            mf_ref[layer, :, q * C : (q + 1) * C] = high
            mf_ref[layer, :, 384 + q * C : 384 + (q + 1) * C] = high
            mf_ref[layer, :, 768 + q * C : 768 + (q + 1) * C] = low
    high, mid, low = split3(emb)
    stack = jnp.concatenate([high.astype(f32), mid.astype(f32), low.astype(f32), jnp.zeros((4, C), f32)], 0)
    et_ref[...] = stack.T
    ro_ref[...] = jnp.broadcast_to(read_ref[...], (C, L)).T
    pick = jnp.where(iota((4, 4), 0) == iota((4, 4), 1), off_ref[...], 0.0)
    eo_ref[...] = jnp.broadcast_to(jnp.sum(pick, 1, keepdims=True), (4, L))


def decode(ids):
    cell = ids >> 3
    ox = (cell >= 9).astype(i32) + (cell >= 18).astype(i32)
    rest = cell - 9 * ox
    oy = (rest >= 3).astype(i32) + (rest >= 6).astype(i32)
    oz = rest - 3 * oy
    lane = lanes(ids.shape)
    ys = (lane >> 6) + oy
    zs = ((lane >> 3) + oz + 7) & 7
    tile = ox * 2 + (ys >> 1)
    target = ((ys & 1) << 6) | (zs << 3) | (ids & 7)
    return ox, oy, oz, tile, target


PX, PY, PZ, RAD, RINV, UM, TM, SP, TILE, TARGET, Y1X, Y1Y, Y1Z, Y20, Y21, Y22, Y23, Y24 = range(18)
COUNTS = (1, 3, 5)
HALF = (1.0,) + (0.5 * R3,) * 3 + (0.5 * R15, 0.5 * R15, 0.5 * R5, 0.5 * R15, 0.5 * R15)


def silu_parts(v):
    gate = 1.0 / (1.0 + jnp.exp(-v))
    return v * gate, gate * (1.0 + v * (1.0 - gate))


def order_of(qm):
    return 0 if qm == 0 else 1 if qm < 4 else 2


def one_hot_block(code16, block):
    spot = (iota((16, L), 0) + 16 * block).astype(f32).astype(bf16)
    return jnp.where(spot == code16, jnp.ones((), bf16), jnp.zeros((), bf16))


def main_kernel(
    lown_ref, rown_ref, froml_ref, fromr_ref,
    vf_ref, vb_ref, wf_ref, wb_ref, mf_ref, mb_ref, et_ref, ro_ref, eo_ref,
    outl_ref, outo_ref, outr_ref,
    table, edges, geo, basis, slope, psplit, moment, zbuf, inv, hid, dsilu, dhid, dmom, geo2,
    rbst, hg, hs, rad2, efac, invx, dha, dhb, dra, drb, dacc, extra, dsplit, force, energy,
):
    for plane, (ref, base) in enumerate(
        ((froml_ref, 0), (froml_ref, 1), (lown_ref, 0), (lown_ref, 1), (fromr_ref, 0), (fromr_ref, 1))
    ):
        for pair in range(3):
            at = (base * 3 + pair) * 4
            table[plane * 3 + pair, 0:4, :] = ref[at : at + 4, :]
    for plane, ref in enumerate((froml_ref, lown_ref, rown_ref, fromr_ref)):
        for r in range(2):
            edges[plane * 2 + r] = ref[24 + 32 * r : 56 + 32 * r, :]

    centre = iota((NB, L), 0).astype(f32) * (CUT / (NB - 1))

    def sums(xr, r):
        at = xr * 2 + r
        base = (xr + 1) * 3 + r
        own = halves(table[base], table[base + 1])
        ids = edges[at, 0:16, :].astype(i32)
        ox, oy, oz, tile, target = decode(ids)
        got = [jnp.zeros((E, L), f32) for _ in range(4)]
        for t in range(6):
            src = table[(xr + t // 2) * 3 + r + t % 2]
            here = tile == t
            for q in range(4):
                wide = jnp.broadcast_to(src[q : q + 1], (E, L))
                val = jnp.take_along_axis(wide, target, axis=1, mode="promise_in_bounds")
                got[q] = jnp.where(here, val, got[q])
        dx = ((ox - 1).astype(f32) + got[0]) - own[0:1]
        dy = ((oy - 1).astype(f32) + got[1]) - own[1:2]
        dz = ((oz - 1).astype(f32) + got[2]) - own[2:3]
        sq = dx * dx + dy * dy + dz * dz
        dist = jnp.sqrt(sq)
        part = jnp.where(dist < CUT, 1.0 - sq * (1.0 / CUT**2), 0.0) * edges[at, 16:32, :]
        px, py, pz = 0.5 * dx, 0.5 * dy, 0.5 * dz
        geo[at, PX] = px
        geo[at, PY] = py
        geo[at, PZ] = pz
        geo[at, RAD] = dist
        geo[at, RINV] = lax.rsqrt(sq)
        geo[at, UM] = part * part
        geo[at, TM] = part
        geo[at, SP] = got[3]
        geo[at, TILE] = tile.astype(f32)
        geo[at, TARGET] = target.astype(f32)
        geo[at, Y1X] = R3 * px
        geo[at, Y1Y] = R3 * py
        geo[at, Y1Z] = R3 * pz
        geo[at, Y20] = R15 * px * py
        geo[at, Y21] = R15 * py * pz
        geo[at, Y22] = (0.5 * R5) * (2.0 * pz * pz - px * px - py * py)
        geo[at, Y23] = R15 * px * pz
        geo[at, Y24] = (0.5 * R15) * (px * px - py * py)

        def row(i, e):
            return jnp.broadcast_to(geo[at, i, e : e + 1, :], (NB, L))

        for e in range(E):
            diff = row(RAD, e) - centre
            bump = jnp.exp(-GAMMA * (diff * diff))
            rb = bump * row(UM, e)
            basis[at, e] = rb
            slope[at, e] = (-2.0) * (bump * row(TM, e)) - (4.0 * GAMMA) * (diff * rb * row(RINV, e))
        acc = [[None] * 4 for _ in range(9)]
        for e in range(E):
            rb = basis[at, e]
            kind = row(SP, e)
            per = [jnp.where(kind == float(k), rb, 0.0) for k in range(4)]
            for qm in range(9):
                y = None if qm == 0 else row(Y1X + qm - 1, e)
                for k in range(4):
                    term = per[k] if y is None else y * per[k]
                    acc[qm][k] = term if e == 0 else acc[qm][k] + term
        for qm in range(9):
            for k in range(4):
                high, low = split2(acc[qm][k])
                psplit[at, qm, k * 8 : k * 8 + 8] = high
                psplit[at, qm, 32 + k * 8 : 40 + k * 8] = low

    def invariants(source, dest, width, xr):
        for i in range(8):
            rows = slice(i * 16, i * 16 + 16)
            first = 0
            for q, count in enumerate(COUNTS):
                value = source(first, rows)
                if q > 0:
                    value = value * value
                    for m in range(1, count):
                        a = source(first + m, rows)
                        value = value + a * a
                first += count
                for r in range(width):
                    high, low = split2(value[:, r * L : (r + 1) * L])
                    dest[r, q * C + i * 16 : q * C + i * 16 + 16] = high
                    dest[r, 384 + q * C + i * 16 : 384 + q * C + i * 16 + 16] = low

    def features(xr):
        for qm in range(9):
            both = jnp.concatenate([psplit[xr * 2, qm], psplit[xr * 2 + 1, qm]], 1)
            moment[xr, qm] = dot(vf_ref[order_of(qm)], jnp.concatenate([both, both[0:32]], 0))
        invariants(lambda qm, rows: moment[xr, qm, rows, :], inv, 2, xr)
        both = jnp.concatenate([inv[0], inv[1]], 1)
        zbuf[0] = dot(mf_ref[0], jnp.concatenate([both, both[0:384]], 0))
        sel = iota((16, L), 0)
        hots = []
        for r in range(2):
            base = (xr + 1) * 3 + r
            own = halves(table[base], table[base + 1])
            kind = jnp.broadcast_to(own[3:4], (16, L))
            hots.append(jnp.where((kind == (sel % 4).astype(f32)) & (sel < 12), 1.0, 0.0))
        zbuf[1] = dot(et_ref[...], jnp.concatenate(hots, 1))
        for i in range(16):
            rows = slice(i * 8, i * 8 + 8)
            update, slope_z = silu_parts(zbuf[0, rows, :])
            h1 = zbuf[1, rows, :] + update
            hid[xr * 2, rows, :] = h1[:, 0:L]
            hid[xr * 2 + 1, rows, :] = h1[:, L:]
            dsilu[xr, rows, :] = slope_z

    def layer_one(xr, _):
        features(xr)
        sums(xr + 1, 0)
        sums(xr + 1, 1)
        return 0

    sums(0, 0)
    sums(0, 1)
    lax.fori_loop(0, 3, layer_one, 0)
    features(3)

    low_half = lanes((C, L)) < 64
    for plane in range(4):
        for r in range(2):
            if plane in (1, 2):
                keep = low_half if r == 1 else ~low_half
                dhid[plane, :, r * L : (r + 1) * L] = jnp.where(keep, ro_ref[...], 0.0)
            else:
                dhid[plane, :, r * L : (r + 1) * L] = jnp.zeros((C, L), f32)
    for r in range(2):
        for e in range(E):
            for i in range(4):
                extra[0, r, e, i] = jnp.zeros((8, L), f32)
    lane8 = lanes((8, L))

    def layer_two(x, _):
        a, b = (x + 1) * 2, (x + 1) * 2 + 1
        ids = halves(edges[a, 0:16, :], edges[b, 0:16, :]).astype(i32)
        _, _, _, tile, target = decode(ids)
        geo2[TILE] = tile.astype(f32)
        geo2[TARGET] = target.astype(f32)
        for i in (PX, PY, PZ, Y1X, Y1Y, Y1Z, Y20, Y21, Y22, Y23, Y24):
            geo2[i] = halves(geo[a, i], geo[b, i])
        for e in range(E):
            rb = halves(basis[a, e], basis[b, e])
            high, low = split2(rb)
            rbst[e] = jnp.concatenate([high, low, high], 0)

        for t in range(6):
            high, low = split2(hid[(x + t // 2) * 2 + t % 2])
            hg[t, 0:128] = high.astype(bf16)
            hg[t, 128:256] = low.astype(bf16)

        def code_row(i, e):
            return jnp.broadcast_to(geo2[i, pl.ds(e, 1), :], (16, L))

        def hot_blocks(pair, which):
            tiles = [code_row(TILE, 2 * pair + half) for half in range(2)]
            spots = [code_row(TARGET, 2 * pair + half) for half in range(2)]
            blocks = []
            for t in which:
                codes = [jnp.where(tiles[i] == float(t), spots[i], -1.0).astype(bf16) for i in range(2)]
                for block in range(8):
                    blocks.append(jnp.concatenate([one_hot_block(code, block) for code in codes], 1))
            return jnp.concatenate(blocks, 0)

        def gather(pair):
            table_x = jnp.concatenate([hg[t] for t in range(6)], 1)
            out = dot(table_x, hot_blocks(pair, range(6)))
            both = jnp.concatenate([rbst[2 * pair], rbst[2 * pair + 1]], 1)
            for half in range(2):
                cols = slice(half * L, (half + 1) * L)
                hs[2 * pair + half] = out[0:128, cols] + out[128:256, cols]
            for q in range(3):
                rad = dot(wf_ref[q], both)
                rad2[2 * pair, q] = rad[:, 0:L]
                rad2[2 * pair + 1, q] = rad[:, L:]

        def contract(pair):
            for i in range(8):
                rows = slice(i * 16, i * 16 + 16)
                acc = [None if pair == 0 else efac[qm, rows, :] for qm in range(9)]
                for e in (2 * pair, 2 * pair + 1):
                    h = hs[e, rows, :]
                    ts = [rad2[e, q, rows, :] * h for q in range(3)]
                    for qm in range(9):
                        if qm == 0:
                            term = ts[0]
                        else:
                            y = jnp.broadcast_to(geo2[Y1X + qm - 1, e : e + 1, :], (16, L))
                            term = y * ts[order_of(qm)]
                        acc[qm] = term if acc[qm] is None else acc[qm] + term
                for qm in range(9):
                    efac[qm, rows, :] = acc[qm] * SCALE if pair == 7 else acc[qm]

        gather(0)
        for pair in range(8):
            if pair < 7:
                gather(pair + 1)
            contract(pair)

        invariants(lambda qm, rows: efac[qm, rows, :], invx, 1, 0)
        zbuf[0, :, 0:L] = dot(mf_ref[1], jnp.concatenate([invx[0], invx[0, 0:384]], 0))
        total = jnp.zeros((8, L), f32)
        for i in range(8):
            rows = slice(i * 16, i * 16 + 16)
            update, slope_z = silu_parts(zbuf[0, rows, 0:L])
            term = ro_ref[rows, :] * (halves(hid[a, rows, :], hid[b, rows, :]) + update)
            total = total + (term[0:8] + term[8:16])
            high, low = split2(ro_ref[rows, :] * slope_z)
            invx[0, i * 16 : i * 16 + 16] = high
            invx[0, 128 + i * 16 : 144 + i * 16] = low
        kind = table[(x + 2) * 3 + 1, 3:4, :]
        offset = jnp.zeros((1, L), f32)
        for k in range(4):
            offset = jnp.where(kind == float(k), eo_ref[k : k + 1, :], offset)
        energy[x] = jnp.broadcast_to(jnp.sum(total, 0, keepdims=True) + offset, (8, L))

        both = jnp.concatenate([invx[0, 0:256], invx[0, 0:128]], 0)
        zbuf[0, :, 0:L] = dot(mb_ref[1, 0:128], both)
        zbuf[0, :, L:] = dot(mb_ref[1, 128:256], both)
        zbuf[1, :, 0:L] = dot(mb_ref[1, 256:384], both)
        for i in range(8):
            rows = slice(i * 16, i * 16 + 16)
            efac[0, rows, :] = zbuf[0, rows, 0:L] * SCALE
            one = zbuf[0, rows, L:] * (2.0 * SCALE)
            two = zbuf[1, rows, 0:L] * (2.0 * SCALE)
            for m in range(1, 9):
                efac[m, rows, :] = efac[m, rows, :] * (one if m < 4 else two)

        def edge_grad(e, dh, dr):
            def row(i, n):
                return jnp.broadcast_to(geo2[i, pl.ds(e, 1), :], (n, L))

            ys = [None] + [row(Y1X + m, 16) for m in range(8)]
            acc = [None] * 9
            for i in range(8):
                rows = slice(i * 16, i * 16 + 16)
                low_rows = slice(128 + i * 16, 144 + i * 16)
                h = hs[e, rows, :]
                rr = [rad2[e, q, rows, :] for q in range(3)]
                ef = [efac[qm, rows, :] for qm in range(9)]
                d0 = ef[0]
                d1 = ys[1] * ef[1] + ys[2] * ef[2] + ys[3] * ef[3]
                d2 = ys[4] * ef[4] + ys[5] * ef[5] + ys[6] * ef[6] + ys[7] * ef[7] + ys[8] * ef[8]
                t1 = rr[1] * h
                t2 = rr[2] * h
                for qm in range(1, 9):
                    term = (t1 if qm < 4 else t2) * ef[qm]
                    term = term[0:8] + term[8:16]
                    acc[qm] = term if i == 0 else acc[qm] + term
                dh[rows], dh[low_rows] = split2(d0 * rr[0] + d1 * rr[1] + d2 * rr[2])
                for q, d in enumerate((d0, d1, d2)):
                    dr[q, rows], dr[q, low_rows] = split2(d * h)
            px, py, pz = (row(i, 8) for i in (PX, PY, PZ))
            gx = R3 * acc[1] + R15 * (py * acc[4] + pz * acc[7] + px * acc[8]) - R5 * (px * acc[6])
            gy = R3 * acc[2] + R15 * (px * acc[4] + pz * acc[5] - py * acc[8]) - R5 * (py * acc[6])
            gz = R3 * acc[3] + R15 * (py * acc[5] + px * acc[7]) + (2.0 * R5) * (pz * acc[6])
            for i, g in enumerate((gx, gy, gz)):
                turned = roll(0.5 * g, 64)
                extra[x + 1, 0, e, i + 1] = jnp.where(lane8 >= 64, turned, 0.0)
                extra[x + 1, 1, e, i + 1] = jnp.where(lane8 < 64, turned, 0.0)
        def spread_back(pair, dh, dr):
            grad = None
            for q in range(3):
                piece = dot(wb_ref[q], jnp.concatenate([dr[0, q], dr[1, q]], 1))
                grad = piece if grad is None else grad + piece
            grad = grad[0:8] + grad[8:16]
            for half in range(2):
                turned = roll(grad[:, half * L : (half + 1) * L], 64)
                extra[x + 1, 0, 2 * pair + half, 0] = jnp.where(lane8 >= 64, turned, 0.0)
                extra[x + 1, 1, 2 * pair + half, 0] = jnp.where(lane8 < 64, turned, 0.0)
            left = jnp.concatenate([dh[0], dh[1]], 1).astype(bf16)

            for part in range(3):
                hot = hot_blocks(pair, (2 * part, 2 * part + 1))
                dacc[part] = dacc[part] + dot(left, hot, ((1,), (1,)))

        for part in range(3):
            dacc[part] = jnp.zeros((256, 256), f32)
        for half in range(2):
            edge_grad(half, dhb.at[half], drb.at[half])

        def back(i, _):
            for half in range(2):
                edge_grad(4 * i + 2 + half, dha.at[half], dra.at[half])
            spread_back(2 * i, dhb, drb)
            for half in range(2):
                edge_grad(4 * i + 4 + half, dhb.at[half], drb.at[half])
            spread_back(2 * i + 1, dha, dra)
            return 0

        lax.fori_loop(0, 3, back, 0)
        for half in range(2):
            edge_grad(14 + half, dha.at[half], dra.at[half])
        spread_back(6, dhb, drb)
        spread_back(7, dha, dra)
        for part in range(3):
            for i in range(8):
                rows = slice(i * 16, i * 16 + 16)
                total = dacc[part, rows, :] + dacc[part, 128 + i * 16 : 144 + i * 16, :]
                dhid[x + part, rows, :] = dhid[x + part, rows, :] + total
        return 0

    lax.fori_loop(0, 2, layer_two, 0)

    def sums_back(xr):
        for i in range(8):
            rows = slice(i * 16, i * 16 + 16)
            value = dhid[xr, rows, :] * dsilu[xr, rows, :]
            for r in range(2):
                high, low = split2(value[:, r * L : (r + 1) * L])
                inv[r, i * 16 : i * 16 + 16] = high
                inv[r, 128 + i * 16 : 144 + i * 16] = low
        both = jnp.concatenate([inv[0, 0:256], inv[1, 0:256]], 1)
        both = jnp.concatenate([both, both[0:128]], 0)
        for q in range(3):
            zbuf[q] = dot(mb_ref[0, q * C : (q + 1) * C], both)
        for i in range(8):
            rows = slice(i * 16, i * 16 + 16)
            parts = [zbuf[0, rows, :], 2.0 * zbuf[1, rows, :], 2.0 * zbuf[2, rows, :]]
            for qm in range(9):
                value = parts[0] if qm == 0 else parts[order_of(qm)] * moment[xr, qm, rows, :]
                for r in range(2):
                    high, low = split2(value[:, r * L : (r + 1) * L])
                    dsplit[qm, r, i * 16 : i * 16 + 16] = high
                    dsplit[qm, r, 128 + i * 16 : 144 + i * 16] = low
        for qm in range(9):
            out = dot(vb_ref[order_of(qm)], jnp.concatenate([dsplit[qm, 0], dsplit[qm, 1]], 1))
            out = HALF[qm] * (out[0:32] + out[32:64])
            dmom[xr * 2, qm] = out[:, 0:L]
            dmom[xr * 2 + 1, qm] = out[:, L:]

    for i in range(18):
        force[i] = jnp.zeros((8, L), f32)
    sub8 = iota((8, L), 0)

    def forces(xr):
        slab = xr % 3 if isinstance(xr, int) else jnp.where((xr == 1) | (xr == 2), xr, 0)
        for r in range(2):
            at = xr * 2 + r
            received = jnp.zeros((8, L), f32)
            picks, hots = [], []
            for e in range(E):
                def row(i):
                    return jnp.broadcast_to(geo[at, i, e : e + 1, :], (NB, L))

                kind = row(SP)
                is0, is1, is2 = kind == 0.0, kind == 1.0, kind == 2.0
                dp = []
                for qm in range(9):
                    sel = jnp.where(is2, dmom[at, qm, 16:24, :], dmom[at, qm, 24:32, :])
                    sel = jnp.where(is1, dmom[at, qm, 8:16, :], sel)
                    dp.append(jnp.where(is0, dmom[at, qm, 0:8, :], sel))
                px, py, pz = row(PX), row(PY), row(PZ)
                dz6 = dp[6] * pz
                gx = dp[1] + py * dp[4] + pz * dp[7] + px * (dp[8] - dp[6])
                gy = dp[2] + px * dp[4] + pz * dp[5] - py * (dp[8] + dp[6])
                gz = dp[3] + py * dp[5] + px * dp[7] + (dz6 + dz6)
                g = dp[0] + px * (gx + dp[1]) + py * (gy + dp[2]) + pz * (gz + dp[3])
                g = g + extra[slab, r, e, 0]
                radial = g * slope[at, e]
                rb = basis[at, e]
                gx = px * radial + rb * gx + extra[slab, r, e, 1]
                gy = py * radial + rb * gy + extra[slab, r, e, 2]
                gz = pz * radial + rb * gz + extra[slab, r, e, 3]
                sx = jnp.sum(gx, 0, keepdims=True)
                sy = jnp.sum(gy, 0, keepdims=True)
                sz = jnp.sum(gz, 0, keepdims=True)
                vec = jnp.where(sub8 == 0, sx, jnp.where(sub8 == 1, sy, jnp.where(sub8 == 2, sz, 0.0)))
                received = received + vec
                both = jnp.concatenate(split2(vec), 0).astype(bf16)
                where_t = jnp.broadcast_to(geo[at, TILE, e : e + 1, :], (16, L)).astype(bf16)
                picks.append(
                    [jnp.where(where_t == jnp.full((), t, bf16), both, jnp.zeros((), bf16)) for t in range(6)]
                )
                code = jnp.broadcast_to(geo[at, TARGET, e : e + 1, :], (16, L)).astype(bf16)
                hots.append([one_hot_block(code, block) for block in range(8)])
                if e % 2:
                    left = jnp.concatenate([jnp.concatenate(p, 0) for p in picks], 1)
                    right = jnp.concatenate([jnp.concatenate(h, 0) for h in hots], 1)
                    piece = dot(left, right, ((1,), (1,)))
                    sent = piece if e == 1 else sent + piece
                    picks, hots = [], []
            for t in range(6):
                to = (xr + t // 2) * 3 + r + t % 2
                force[to] = force[to] - (sent[t * 16 : t * 16 + 8] + sent[t * 16 + 8 : t * 16 + 16])
            turned = roll(received, 64)
            mine = (xr + 1) * 3 + r
            force[mine] = force[mine] + jnp.where(lane8 >= 64, turned, 0.0)
            force[mine + 1] = force[mine + 1] + jnp.where(lane8 < 64, turned, 0.0)

    def layer_one_back(xr, _):
        sums_back(xr + 1)
        forces(xr)
        return 0

    sums_back(0)
    lax.fori_loop(0, 3, layer_one_back, 0)
    forces(3)

    for plane in range(6):
        for pair in range(3):
            out = (outl_ref, outo_ref, outr_ref)[plane // 2]
            at = ((plane % 2) * 3 + pair) * 4
            out[at : at + 4, :] = force[plane * 3 + pair, 0:4, :]
            if plane in (2, 3) and pair == 1:
                out[at + 3 : at + 4, :] = energy[plane - 2, 0:1, :]


def chunk_kernel(gy_ref, gz_ref, own_ref, left_ref, right_ref, out_ref):
    gy, gz = gy_ref[0], gz_ref[0]
    front = gz == 0
    total = own_ref[...] + left_ref[...] + right_ref[...]
    quarter = lanes((4, L)) // 32

    def squeeze(pair, zh):
        first = total[pair * 4 : pair * 4 + 4]
        second = total[12 + pair * 4 : 16 + pair * 4]
        out = roll(first, -32 * zh)
        out = jnp.where(quarter == 1, roll(first, -32 - 32 * zh), out)
        out = jnp.where(quarter == 2, roll(second, 64 - 32 * zh), out)
        return jnp.where(quarter == 3, roll(second, 32 - 32 * zh), out)

    out_ref[...] = jnp.zeros(out_ref.shape, f32)
    y_count = out_ref.shape[0] // 2
    beside = jnp.where(front, gy + y_count - 1, gy + 1)
    beside = jnp.where(beside >= y_count, beside - y_count, beside)
    for zh in range(2):
        parts = [squeeze(pair, zh) for pair in range(3)]
        low = jnp.where(front, parts[1], parts[0])
        high = jnp.where(front, parts[2], parts[1])
        near = jnp.where(front, parts[0], parts[2])
        out_ref[gy * 2 + zh] = jnp.concatenate([low, high], 0)
        out_ref[beside * 2 + zh, 0:4, :] = near


def unpack_kernel(gy_ref, got_ref, energy_ref, force_ref):
    gy = gy_ref[0]
    y_count = got_ref.shape[0] // 2
    below = jnp.where(gy == 0, y_count - 1, gy - 1)
    above = jnp.where(gy == y_count - 1, 0, gy + 1)
    own = got_ref[gy * 2] + got_ref[gy * 2 + 1]
    low = own[0:4] + got_ref[below * 2 + 1, 0:4, :]
    high = own[4:8] + got_ref[above * 2, 0:4, :]
    lower = lanes((4, L)) < 64
    first = jnp.where(lower, low, roll(high, 64))
    second = jnp.where(lower, roll(low, 64), high)
    rows = jnp.concatenate([first, second], 1)
    keep, spread8 = block_masks(3)
    group = jnp.where((iota((96, 8), 0) // 4) % 3 == iota((96, 8), 1), 1.0, 0.0).astype(bf16)
    rows8 = jnp.concatenate([rows, jnp.zeros((4, 256), f32)], 0)
    nt = ((1,), (1,))
    total = None
    for part in split3(rows8):
        wide = jnp.where(keep, dot(group, part), 0.0).astype(bf16)
        piece = dot(wide, spread8, nt)
        total = piece if total is None else total + piece
    force_ref[...] = total
    keep, _ = block_masks(1)
    total = None
    for part in split3(rows[3:4]):
        wide = jnp.where(keep, part.astype(f32), 0.0).astype(bf16)
        piece = dot(wide, spread8, nt)
        total = piece if total is None else total + piece
    energy_ref[...] = total


def call(kernel, outs, in_specs, scratch=(), flops=10**6, vmem=4):
    return pl.pallas_call(
        kernel,
        out_shape=outs,
        in_specs=in_specs,
        out_specs=jax.tree.map(lambda _: pl.BlockSpec(memory_space=VMEM), outs),
        scratch_shapes=list(scratch),
        compiler_params=pltpu.CompilerParams(vmem_limit_bytes=int(vmem * 2**20)),
        cost_estimate=pl.CostEstimate(flops=flops, bytes_accessed=10**5, transcendentals=0),
    )


def shape(*dims, dtype=f32):
    return jax.ShapeDtypeStruct(dims, dtype)


def shards(
    positions, species, neighbors, edge_mask, species_embed, radial_weight, mix_weight, readout, energy_offset
):
    v = pl.BlockSpec(memory_space=VMEM)
    sm = pl.BlockSpec(memory_space=SMEM)
    gy_count, gz_count = lax.axis_size("gy"), lax.axis_size("gz")
    gx_count = lax.axis_size("gx")
    gy, gz = lax.axis_index("gy"), lax.axis_index("gz")
    gy_only = gy.astype(i32).reshape(1)
    gz_only = gz.astype(i32).reshape(1)

    own, straight, cross = call(
        pack_kernel,
        [shape(40, 256), shape(40, L), shape(40, L)],
        [sm] + [pl.BlockSpec(memory_space=pltpu.HBM)] * 4,
        [VMEM((96, 8), f32), VMEM((32, 8), i32), VMEM((256, E), i32), VMEM((256, E), i32), pltpu.SemaphoreType.DMA((4,))],
        vmem=53.8,
    )(
        gz_only,
        positions.transpose(0, 1, 4, 2, 3).reshape(96, 8),
        species.reshape(32, 8),
        neighbors.reshape(256, E),
        edge_mask.reshape(256, E),
    )

    def dev(y, s):
        return (y % gy_count) * gz_count + s

    yz = ("gy", "gz")
    go_straight = [(dev(y, s), dev(y + 1 if s == 0 else y - 1, s)) for y in range(gy_count) for s in range(2)]
    go_cross = [(dev(y, s), dev(y - 1 if s == 0 else y + 1, 1 - s)) for y in range(gy_count) for s in range(2)]
    near_straight = lax.ppermute(straight, yz, go_straight)
    near_cross = lax.ppermute(cross, yz, go_cross)
    both = lax.all_gather(own, "gz")

    left, right = call(rows_kernel, [shape(88, L), shape(88, L)], [sm, v, v, v])(
        gz_only, both, near_straight, near_cross
    )
    up = [(i, (i + 1) % gx_count) for i in range(gx_count)]
    down = [(j, i) for i, j in up]
    from_left = lax.ppermute(right, "gx", up)
    from_right = lax.ppermute(left, "gx", down)

    weights = call(
        weights_kernel,
        [
            shape(3, C, 96),
            shape(3, 64, 256),
            shape(3, C, 24),
            shape(3, 16, 256),
            shape(2, C, 1152),
            shape(2, 384, 384),
            shape(C, 16),
            shape(C, L),
            shape(4, L),
        ],
        [v] * 5,
        flops=10**7,
        vmem=8,
    )(species_embed, radial_weight, mix_weight, readout.reshape(1, C), energy_offset.reshape(1, 4))

    scratch = [
        VMEM((18, 8, L), f32),
        VMEM((8, 32, L), f32),
        VMEM((8, 18, E, L), f32),
        VMEM((8, E, NB, L), f32),
        VMEM((8, E, NB, L), f32),
        VMEM((8, 9, 64, L), f32),
        VMEM((4, 9, C, 2 * L), f32),
        VMEM((3, C, 2 * L), f32),
        VMEM((2, 768, L), f32),
        VMEM((8, C, L), f32),
        VMEM((4, C, 2 * L), f32),
        VMEM((4, C, 2 * L), f32),
        VMEM((8, 9, 32, L), f32),
        VMEM((18, E, L), f32),
        VMEM((E, 24, L), f32),
        VMEM((6, 256, L), bf16),
        VMEM((E, C, L), f32),
        VMEM((E, 3, C, L), f32),
        VMEM((9, C, L), f32),
        VMEM((1, 768, L), f32),
        VMEM((2, 256, L), f32),
        VMEM((2, 256, L), f32),
        VMEM((2, 3, 256, L), f32),
        VMEM((2, 3, 256, L), f32),
        VMEM((3, 256, 256), f32),
        VMEM((3, 2, E, 4, 8, L), f32),
        VMEM((9, 2, 256, L), f32),
        VMEM((18, 8, L), f32),
        VMEM((2, 8, L), f32),
    ]
    out_left, out_own, out_right = call(
        main_kernel, [shape(24, L)] * 3, [v] * 13, scratch, flops=10**9, vmem=48
    )(left, right, from_left, from_right, *weights)

    back_right = lax.ppermute(out_left, "gx", down)
    back_left = lax.ppermute(out_right, "gx", up)
    chunks = call(chunk_kernel, shape(gy_count * 2, 8, L), [sm, sm, v, v, v])(gy_only, gz_only, out_own, back_left, back_right)
    got = lax.all_to_all(chunks, yz, 0, 0)
    energy, force = call(unpack_kernel, [shape(32, 8), shape(96, 8)], [sm, v])(gy_only, got)
    return energy.reshape(2, 4, 4, 8), force.reshape(2, 4, 3, 4, 8).transpose(0, 1, 3, 4, 2)


def solution(mesh):
    in_specs = (
        P("gx", "gy", "gz", None, None),
        P("gx", "gy", "gz", None),
        P("gx", "gy", "gz", None, None),
        P("gx", "gy", "gz", None, None),
        P(),
        P(),
        P(),
        P(),
        P(),
    )
    out_specs = (P("gx", "gy", "gz", None), P("gx", "gy", "gz", None, None))
    return jax.shard_map(shards, mesh=mesh, in_specs=in_specs, out_specs=out_specs, check_vma=False)
```

time: 101 us -> 90.9 us (0.900)
  Pallas kernels: 34.9 us -> 25 us
  waiting for transfers between devices: 5.82 us -> 2.68 us
  local copies, waits for them, and re-layouts: 1.4 us -> 4.43 us
    pallas_call x1, Pallas kernels: 31.7 us -> 21.7 us  [shards(): call(main_kernel, [shape(24, L)] * 3, [v] * 13, scratch, flops=10 ** 9, v...]
    ppermute x1, waiting for transfers between devices: 5.02 us -> 1.88 us  [shards(): from_left = lax.ppermute(right, 'gx', up)]
    unnamed x12, local copies, waits for them, and re-layouts: 1.4 us -> 4.43 us
  transfers between devices with their start and end apart: 6 -> 6, of which waited for: 2 -> 2; matrix products, arithmetic and copies ran while one was open for 0% -> 0% of each run, Pallas kernels for 0% -> 1%
where the time goes in v3:
time: 90.9 us; the launch traced here: 90.4 us
  starting transfers between devices  33.7 us (37%)
  Pallas kernels  25 us (28%)
  blocking collectives  23.7 us (26%)
  local copies, waits for them, and re-layouts  4.43 us (5%)
  waiting for transfers between devices  2.68 us (3%)
    pallas_call x1, Pallas kernels, shards(): call(main_kernel, [shape(24, L)] * 3, [v] * 13, scratch, flops=10 ** 9, v...  21.7 us
    all_to_all x1, blocking collectives, shards(): got = lax.all_to_all(chunks, yz, 0, 0)  13.3 us
    ppermute x1, starting transfers between devices, shards(): from_right = lax.ppermute(left, 'gx', down)  12.1 us
    all_gather x1, blocking collectives, shards(): both = lax.all_gather(own, 'gz')  10.4 us
    ppermute x1, starting transfers between devices, shards(): back_right = lax.ppermute(out_left, 'gx', down)  6.68 us
    ppermute x1, starting transfers between devices, shards(): near_cross = lax.ppermute(cross, yz, go_cross)  6.5 us
    ppermute x1, starting transfers between devices, shards(): near_straight = lax.ppermute(straight, yz, go_straight)  4.59 us
    unnamed x12, local copies, waits for them, and re-layouts  4.43 us
  transfers between devices with their start and end apart: 6, of which 2 were waited for; matrix products, arithmetic and copies ran while one was open for 0% of the time, Pallas kernels for 1%

profile of v3, /device:TPU:1, one launch (start us, length us, event | category | flops | bytes accessed | tf_op | source)
XLA Modules:
  0.0 90.4 jit_solution(11815709854283947935)
XLA Ops:
  0.6 0.7 copy-done.2
  1.4 1.4 %shard_map.104 = (f32[40,256]{1,0:T(8,128)S(1)}, f32[40,128]{1,0:T(8,128)S(1)}, f32[40,128]{1,0:T(8,128)S(1)}) custom-call(s32[1]{0:T(128)} %bitcast.1.gz_ref, f32[96,8]{1,0:T(8,128)} %bitcast.21, s32[32,8]{1,0:T(8,128)S(1)} %bitcast.16, s32[256,16]{1,0:T(8,128)} %bitcast.19, s32[256,16]{1,0:T(8,128)} %bitcast.20), custom_call_target="tpu_custom_call" | custom-call | flops 1000000 | bytes 100000 | tf_op jit(solution)/shard_map/pallas_call | solution.py:717
  2.8 4.6 %collective-permute-start = (f32[40,128]{1,0:T(8,128)S(1)}, f32[40,128]{1,0:T(8,128)S(1)}, u32[]{:S(2)}, u32[]{:S(2)}) collective-permute-start(f32[40,128]{1,0:T(8,128)S(1)} %get-tuple-element.22), channel_id=1, source_target_pairs={{0,2},{1,15},{2,4},{3,1},{4,6},{5,3},{6,8},{7,5},{8,10},{9,7},{10,... | collective-permute-start | bytes 61448 | tf_op jit(solution)/shard_map/ppermute | solution.py:737
  7.4 6.5 %collective-permute-start.1 = (f32[40,128]{1,0:T(8,128)S(1)}, f32[40,128]{1,0:T(8,128)S(1)}, u32[]{:S(2)}, u32[]{:S(2)}) collective-permute-start(f32[40,128]{1,0:T(8,128)S(1)} %get-tuple-element.23), channel_id=1, source_target_pairs={{0,15},{1,2},{2,1},{3,4},{4,3},{5,6},{6,5},{7,8},{8,7},{9,10},{10,... | collective-permute-start | bytes 61448 | tf_op jit(solution)/shard_map/ppermute | solution.py:738
  13.9 10.4 %all-gather = f32[80,256]{1,0:T(8,128)S(1)} all-gather(f32[40,256]{1,0:T(8,128)S(1)} %get-tuple-element.21), channel_id=2, replica_groups=mesh['gx'=32,'gy'=8,'gz'=2] {'gz'}, dimensions={0}, use_global_device_ids=true | all-gather | bytes 122880 | tf_op jit(solution)/shard_map/all_gather | solution.py:739
  24.3 0.0 collective-permute-done.straight_ref
  24.3 0.2 shard_map.105
  24.6 12.1 %collective-permute-start.3 = (f32[88,128]{1,0:T(8,128)S(1)}, f32[88,128]{1,0:T(8,128)S(1)}, u32[]{:S(2)}, u32[]{:S(2)}) collective-permute-start(f32[88,128]{1,0:T(8,128)S(1)} %get-tuple-element.24.lown_ref), channel_id=1, source_target_pairs={{16,0},{32,16},{48,32},{64,48},{80,64},{96,80},{112,96},{128,112},... | collective-permute-start | bytes 135176 | tf_op jit(solution)/shard_map/ppermute | solution.py:747
  36.7 1.9 %collective-permute-start.2 = (f32[88,128]{1,0:T(8,128)S(1)}, f32[88,128]{1,0:T(8,128)S(1)}, u32[]{:S(2)}, u32[]{:S(2)}) collective-permute-start(f32[88,128]{1,0:T(8,128)S(1)} %get-tuple-element.25.rown_ref), channel_id=1, source_target_pairs={{0,16},{16,32},{32,48},{48,64},{64,80},{80,96},{96,112},{112,128},... | collective-permute-start | bytes 135176 | tf_op jit(solution)/shard_map/ppermute | solution.py:746
  38.6 0.0 copy-start
  38.6 1.0 %copy-done = f32[2,384,128]{2,1,0:T(8,128)S(1)} copy-done((f32[2,384,128]{2,1,0:T(8,128)S(1)}, f32[2,384,128]{2,1,0:T(8,128)}, u32[]{:S(2)}) %copy-start) | copy-done | bytes 393240
  39.6 0.7 copy-done.1
  40.4 0.7 copy-done.3
  41.0 0.7 copy-done.4
  41.7 0.7 copy-done.5
  42.3 0.6 shard_map.106
  42.9 1.9 %collective-permute-done.2.froml_ref = f32[88,128]{1,0:T(8,128)S(1)} collective-permute-done((f32[88,128]{1,0:T(8,128)S(1)}, f32[88,128]{1,0:T(8,128)S(1)}, u32[]{:S(2)}, u32[]{:S(2)}) %collective-permute-start.2) | collective-permute-done | bytes 45088 | tf_op jit(solution)/shard_map/ppermute | solution.py:746
  44.8 21.7 %shard_map.107 = (f32[24,128]{1,0:T(8,128)S(1)}, f32[24,128]{1,0:T(8,128)S(1)}, f32[24,128]{1,0:T(8,128)S(1)}) custom-call(f32[88,128]{1,0:T(8,128)S(1)} %get-tuple-element.24.lown_ref, f32[88,128]{1,0:T(8,128)S(1)} %get-tuple-element.25.rown_ref, f32[88,128]{1,0:T(8,128)S(1)} %collective-permute-done.2.froml_ref, ...), custom_call_target="tpu_custom_call" | custom-call | flops 1000000000 | bytes 100000 | tf_op jit(solution)/shard_map/pallas_call | solution.py:798
  66.5 1.9 %collective-permute-start.4 = (f32[24,128]{1,0:T(8,128)S(1)}, f32[24,128]{1,0:T(8,128)S(1)}, u32[]{:S(2)}, u32[]{:S(2)}) collective-permute-start(f32[24,128]{1,0:T(8,128)S(1)} %get-tuple-element.36), channel_id=1, source_target_pairs={{0,16},{16,32},{32,48},{48,64},{64,80},{80,96},{96,112},{112,128},... | collective-permute-start | bytes 36872 | tf_op jit(solution)/shard_map/ppermute | solution.py:803
  68.5 6.7 %collective-permute-start.5 = (f32[24,128]{1,0:T(8,128)S(1)}, f32[24,128]{1,0:T(8,128)S(1)}, u32[]{:S(2)}, u32[]{:S(2)}) collective-permute-start(f32[24,128]{1,0:T(8,128)S(1)} %get-tuple-element.37), channel_id=1, source_target_pairs={{16,0},{32,16},{48,32},{64,48},{80,64},{96,80},{112,96},{128,112},... | collective-permute-start | bytes 36872 | tf_op jit(solution)/shard_map/ppermute | solution.py:802
  75.2 0.8 collective-permute-done.5.right_ref
  76.0 0.1 shard_map.108
  76.1 13.3 %all_to_all.5.got_ref = f32[16,8,128]{2,1,0:T(8,128)S(1)} all-to-all(f32[16,8,128]{2,1,0:T(8,128)S(1)} %shard_map.108), channel_id=1, replica_groups=mesh['gx'=32,'gy'=8,'gz'=2] {'gy','gz'}, dimensions={0} | all-to-all | bytes 131072 | tf_op jit(solution)/shard_map/all_to_all | solution.py:805
  89.4 1.0 %shard_map.109 = (f32[32,8]{1,0:T(8,128)}, f32[96,8]{1,0:T(8,128)}) custom-call(s32[1]{0:T(128)} %bitcast.gy_ref, f32[16,8,128]{2,1,0:T(8,128)S(1)} %all_to_all.5.got_ref), custom_call_target="tpu_custom_call" | custom-call | flops 1000000 | bytes 100000 | tf_op jit(solution)/shard_map/pallas_call | solution.py:806
  (8 shorter events, 0.0 us)
Async XLA Ops:
  0.6 0.7 copy-start.2
  2.8 21.6 %collective-permute-start = (f32[40,128]{1,0:T(8,128)S(1)}, f32[40,128]{1,0:T(8,128)S(1)}, u32[]{:S(2)}, u32[]{:S(2)}) collective-permute-start(f32[40,128]{1,0:T(8,128)S(1)} %get-tuple-element.22), channel_id=1, source_target_pairs={{0,2},{1,15},{2,4},{3,1},{4,6},{5,3},{6,8},{7,5},{8,10},{9,7},{10,... | collective-permute-start | bytes 61448 | tf_op jit(solution)/shard_map/ppermute | solution.py:737
  7.4 17.0 %collective-permute-start.1 = (f32[40,128]{1,0:T(8,128)S(1)}, f32[40,128]{1,0:T(8,128)S(1)}, u32[]{:S(2)}, u32[]{:S(2)}) collective-permute-start(f32[40,128]{1,0:T(8,128)S(1)} %get-tuple-element.23), channel_id=1, source_target_pairs={{0,15},{1,2},{2,1},{3,4},{4,3},{5,6},{6,5},{7,8},{8,7},{9,10},{10,... | collective-permute-start | bytes 61448 | tf_op jit(solution)/shard_map/ppermute | solution.py:738
  24.6 18.4 %collective-permute-start.3 = (f32[88,128]{1,0:T(8,128)S(1)}, f32[88,128]{1,0:T(8,128)S(1)}, u32[]{:S(2)}, u32[]{:S(2)}) collective-permute-start(f32[88,128]{1,0:T(8,128)S(1)} %get-tuple-element.24.lown_ref), channel_id=1, source_target_pairs={{16,0},{32,16},{48,32},{64,48},{80,64},{96,80},{112,96},{128,112},... | collective-permute-start | bytes 135176 | tf_op jit(solution)/shard_map/ppermute | solution.py:747
  36.7 8.1 %collective-permute-start.2 = (f32[88,128]{1,0:T(8,128)S(1)}, f32[88,128]{1,0:T(8,128)S(1)}, u32[]{:S(2)}, u32[]{:S(2)}) collective-permute-start(f32[88,128]{1,0:T(8,128)S(1)} %get-tuple-element.25.rown_ref), channel_id=1, source_target_pairs={{0,16},{16,32},{32,48},{48,64},{64,80},{80,96},{96,112},{112,128},... | collective-permute-start | bytes 135176 | tf_op jit(solution)/shard_map/ppermute | solution.py:746
  38.6 1.0 %copy-start = (f32[2,384,128]{2,1,0:T(8,128)S(1)}, f32[2,384,128]{2,1,0:T(8,128)}, u32[]{:S(2)}) copy-start(f32[2,384,128]{2,1,0:T(8,128)} %mix_ref.1) | copy-start | bytes 1179652
  39.6 0.7 copy-start.1
  40.4 0.7 copy-start.3
  41.0 0.7 copy-start.4
  41.7 0.7 copy-start.5
  66.5 8.6 %collective-permute-start.4 = (f32[24,128]{1,0:T(8,128)S(1)}, f32[24,128]{1,0:T(8,128)S(1)}, u32[]{:S(2)}, u32[]{:S(2)}) collective-permute-start(f32[24,128]{1,0:T(8,128)S(1)} %get-tuple-element.36), channel_id=1, source_target_pairs={{0,16},{16,32},{32,48},{48,64},{64,80},{80,96},{96,112},{112,128},... | collective-permute-start | bytes 36872 | tf_op jit(solution)/shard_map/ppermute | solution.py:803
  68.5 7.5 %collective-permute-start.5 = (f32[24,128]{1,0:T(8,128)S(1)}, f32[24,128]{1,0:T(8,128)S(1)}, u32[]{:S(2)}, u32[]{:S(2)}) collective-permute-start(f32[24,128]{1,0:T(8,128)S(1)} %get-tuple-element.37), channel_id=1, source_target_pairs={{16,0},{32,16},{48,32},{64,48},{80,64},{96,80},{112,96},{128,112},... | collective-permute-start | bytes 36872 | tf_op jit(solution)/shard_map/ppermute | solution.py:802

commit v4 on v3

--- a/solution.py
+++ b/solution.py
@@ -6,6 +6,7 @@
 from jax.experimental import pallas as pl
 from jax.experimental.pallas import tpu as pltpu
 from jax.sharding import PartitionSpec as P
+
 
 f32 = jnp.float32
 bf16 = jnp.bfloat16
@@ -18,6 +19,7 @@
 CUT = 2.0
 GAMMA = ((NB - 1) / CUT) ** 2
 SCALE = E**-0.5
+PACK_VMEM = 4
 R3 = math.sqrt(3.0)
 R5 = math.sqrt(5.0)
 R15 = math.sqrt(15.0)
@@ -61,17 +63,18 @@
 
 
 def pack_kernel(
-    gz_ref, pos_hbm, spec_hbm, nbr_hbm, mask_hbm, own_ref, straight_ref, cross_ref, pos_ref, spec_ref, nbr_ref, mask_ref, sems
+    gz_ref, pos_hbm, spec_hbm, nbr_hbm, mask_hbm, emb_hbm, rad_hbm, mix_hbm, read_hbm, off_hbm,
+    own_ref, straight_ref, cross_ref, emb_ref, rad_ref, mix_ref, read_ref, off_ref,
+    pos_ref, spec_ref, nbr_ref, mask_ref, sems,
 ):
-    copies = [
-        pltpu.make_async_copy(src, dst, sems.at[i])
-        for i, (src, dst) in enumerate(
-            ((nbr_hbm, nbr_ref), (mask_hbm, mask_ref), (pos_hbm, pos_ref), (spec_hbm, spec_ref))
-        )
-    ]
+    pairs = (
+        (nbr_hbm, nbr_ref), (mask_hbm, mask_ref), (pos_hbm, pos_ref), (spec_hbm, spec_ref),
+        (emb_hbm, emb_ref), (rad_hbm, rad_ref), (mix_hbm, mix_ref), (read_hbm, read_ref), (off_hbm, off_ref),
+    )
+    copies = [pltpu.make_async_copy(src, dst, sems.at[i]) for i, (src, dst) in enumerate(pairs)]
     for copy in copies:
         copy.start()
-    for copy in copies:
+    for copy in copies[:4]:
         copy.wait()
     eye16 = jnp.where(iota((E, E), 0) == iota((E, E), 1), 1.0, 0.0).astype(bf16)
     own_ref[0:16, :] = dot(eye16, nbr_ref[...].astype(f32).astype(bf16), ((1,), (1,)))
@@ -95,6 +98,8 @@
     front = gz_ref[0] == 0
     straight_ref[...] = jnp.where(front, rows_high, rows_low)
     cross_ref[...] = jnp.where(front, rows_low, rows_high)
+    for copy in copies[4:]:
+        copy.wait()
 
 
 def spread(half0, half1, start):
@@ -109,14 +114,15 @@
     return roll(jnp.where(lanes(first.shape) >= 64, first, second), 64)
 
 
-def rows_kernel(gz_ref, all_ref, straight_ref, cross_ref, left_ref, right_ref):
+def rows_kernel(gz_ref, other_ref, own_ref, straight_ref, cross_ref, left_ref, right_ref):
     front = gz_ref[0] == 0
+    all_ref = [jnp.where(front, own_ref[...], other_ref[...]), jnp.where(front, other_ref[...], own_ref[...])]
     near0 = jnp.where(front, straight_ref[...], cross_ref[...])
     near1 = jnp.where(front, cross_ref[...], straight_ref[...])
     for x in range(2):
         near = spread(near0, near1, 64 * x)
         own = [
-            spread(all_ref[0, :, x * L : (x + 1) * L], all_ref[1, :, x * L : (x + 1) * L], 64 * pair)
+            spread(all_ref[0][:, x * L : (x + 1) * L], all_ref[1][:, x * L : (x + 1) * L], 64 * pair)
             for pair in range(2)
         ]
         tiles = [
@@ -289,7 +295,7 @@
                 psplit[at, qm, k * 8 : k * 8 + 8] = high
                 psplit[at, qm, 32 + k * 8 : 40 + k * 8] = low
 
-    def invariants(source, dest, width, xr):
+    def invariants(source, dest, width):
         for i in range(8):
             rows = slice(i * 16, i * 16 + 16)
             first = 0
@@ -310,7 +316,7 @@
         for qm in range(9):
             both = jnp.concatenate([psplit[xr * 2, qm], psplit[xr * 2 + 1, qm]], 1)
             moment[xr, qm] = dot(vf_ref[order_of(qm)], jnp.concatenate([both, both[0:32]], 0))
-        invariants(lambda qm, rows: moment[xr, qm, rows, :], inv, 2, xr)
+        invariants(lambda qm, rows: moment[xr, qm, rows, :], inv, 2)
         both = jnp.concatenate([inv[0], inv[1]], 1)
         zbuf[0] = dot(mf_ref[0], jnp.concatenate([both, both[0:384]], 0))
         sel = iota((16, L), 0)
@@ -420,7 +426,7 @@
                 gather(pair + 1)
             contract(pair)
 
-        invariants(lambda qm, rows: efac[qm, rows, :], invx, 1, 0)
+        invariants(lambda qm, rows: efac[qm, rows, :], invx, 1)
         zbuf[0, :, 0:L] = dot(mf_ref[1], jnp.concatenate([invx[0], invx[0, 0:384]], 0))
         total = jnp.zeros((8, L), f32)
         for i in range(8):
@@ -481,6 +487,7 @@
                 turned = roll(0.5 * g, 64)
                 extra[x + 1, 0, e, i + 1] = jnp.where(lane8 >= 64, turned, 0.0)
                 extra[x + 1, 1, e, i + 1] = jnp.where(lane8 < 64, turned, 0.0)
+
         def spread_back(pair, dh, dr):
             grad = None
             for q in range(3):
@@ -714,18 +721,29 @@
     gy_only = gy.astype(i32).reshape(1)
     gz_only = gz.astype(i32).reshape(1)
 
-    own, straight, cross = call(
+    own, straight, cross, *raw = call(
         pack_kernel,
-        [shape(40, 256), shape(40, L), shape(40, L)],
-        [sm] + [pl.BlockSpec(memory_space=pltpu.HBM)] * 4,
-        [VMEM((96, 8), f32), VMEM((32, 8), i32), VMEM((256, E), i32), VMEM((256, E), i32), pltpu.SemaphoreType.DMA((4,))],
-        vmem=53.8,
+        [shape(40, 256), shape(40, L), shape(40, L)]
+        + [shape(4, C), shape(2, NB, 384), shape(2, 384, C), shape(1, C), shape(1, 4)],
+        [sm] + [pl.BlockSpec(memory_space=pltpu.HBM)] * 9,
+        [VMEM((96, 8), f32), VMEM((32, 8), i32), VMEM((256, E), i32), VMEM((256, E), i32), pltpu.SemaphoreType.DMA((9,))],
+        vmem=PACK_VMEM,
     )(
         gz_only,
-        positions.transpose(0, 1, 4, 2, 3).reshape(96, 8),
-        species.reshape(32, 8),
-        neighbors.reshape(256, E),
-        edge_mask.reshape(256, E),
+        *(
+            pltpu.with_memory_space_constraint(x, pltpu.HBM)
+            for x in (
+                positions.transpose(0, 1, 4, 2, 3).reshape(96, 8),
+                species.reshape(32, 8),
+                neighbors.reshape(256, E),
+                edge_mask.reshape(256, E),
+                species_embed,
+                radial_weight,
+                mix_weight,
+                readout.reshape(1, C),
+                energy_offset.reshape(1, 4),
+            )
+        ),
     )
 
     def dev(y, s):
@@ -736,10 +754,10 @@
     go_cross = [(dev(y, s), dev(y - 1 if s == 0 else y + 1, 1 - s)) for y in range(gy_count) for s in range(2)]
     near_straight = lax.ppermute(straight, yz, go_straight)
     near_cross = lax.ppermute(cross, yz, go_cross)
-    both = lax.all_gather(own, "gz")
-
-    left, right = call(rows_kernel, [shape(88, L), shape(88, L)], [sm, v, v, v])(
-        gz_only, both, near_straight, near_cross
+    both = lax.ppermute(own, "gz", [(0, 1), (1, 0)])
+
+    left, right = call(rows_kernel, [shape(88, L), shape(88, L)], [sm, v, v, v, v])(
+        gz_only, both, own, near_straight, near_cross
     )
     up = [(i, (i + 1) % gx_count) for i in range(gx_count)]
     down = [(j, i) for i, j in up]
@@ -762,7 +780,7 @@
         [v] * 5,
         flops=10**7,
         vmem=8,
-    )(species_embed, radial_weight, mix_weight, readout.reshape(1, C), energy_offset.reshape(1, 4))
+    )(*raw)
 
     scratch = [
         VMEM((18, 8, L), f32),

time: 90.9 us -> 84.9 us (0.934)
  blocking collectives: 23.7 us -> 13.3 us
  starting transfers between devices: 33.7 us -> 41.8 us
  local copies, waits for them, and re-layouts: 4.43 us -> 0 us
  waiting for transfers between devices: 2.68 us -> 3.63 us
    all_gather x1 -> x0, blocking collectives: 10.4 us -> none  [shards(): both = lax.all_gather(own, 'gz')]
    ppermute x0 -> x1, starting transfers between devices: none -> 8.27 us  [shards(): both = lax.ppermute(own, 'gz', [(0, 1), (1, 0)])]
    unnamed x12 -> x0, local copies, waits for them, and re-layouts: 4.43 us -> none
    ppermute x1, waiting for transfers between devices: 0.01 us -> 2.29 us  [shards(): near_cross = lax.ppermute(cross, yz, go_cross)]
    ppermute x1, starting transfers between devices: 1.92 us -> 4 us  [shards(): from_left = lax.ppermute(right, 'gx', up)]
    ppermute x1, waiting for transfers between devices: 1.88 us -> 0.01 us  [shards(): from_left = lax.ppermute(right, 'gx', up)]
    ppermute x1, starting transfers between devices: 4.59 us -> 3.15 us  [shards(): near_straight = lax.ppermute(straight, yz, go_straight)]
    ppermute x1, starting transfers between devices: 12.1 us -> 10.8 us  [shards(): from_right = lax.ppermute(left, 'gx', down)]
  transfers between devices with their start and end apart: 6 -> 7, of which waited for: 2 -> 3; matrix products, arithmetic and copies ran while one was open for 0% -> 0% of each run, Pallas kernels for 1% -> 1%
where the time goes in v4:
time: 84.9 us; the launch traced here: 84.6 us
  starting transfers between devices  41.8 us (49%)
  Pallas kernels  25.1 us (30%)
  blocking collectives  13.3 us (16%)
  waiting for transfers between devices  3.63 us (4%)
    pallas_call x1, Pallas kernels, shards(): call(main_kernel, [shape(24, L)] * 3, [v] * 13, scratch, flops=10 ** 9, v...  21.7 us
    all_to_all x1, blocking collectives, shards(): got = lax.all_to_all(chunks, yz, 0, 0)  13.3 us
    ppermute x1, starting transfers between devices, shards(): from_right = lax.ppermute(left, 'gx', down)  10.8 us
    ppermute x1, starting transfers between devices, shards(): both = lax.ppermute(own, 'gz', [(0, 1), (1, 0)])  8.27 us
    ppermute x1, starting transfers between devices, shards(): back_right = lax.ppermute(out_left, 'gx', down)  6.99 us
    ppermute x1, starting transfers between devices, shards(): near_cross = lax.ppermute(cross, yz, go_cross)  6.7 us
    ppermute x1, starting transfers between devices, shards(): from_left = lax.ppermute(right, 'gx', up)  4 us
    ppermute x1, starting transfers between devices, shards(): near_straight = lax.ppermute(straight, yz, go_straight)  3.15 us
  transfers between devices with their start and end apart: 7, of which 3 were waited for; matrix products, arithmetic and copies ran while one was open for 0% of the time, Pallas kernels for 1%

profile of v4, /device:TPU:1, one launch (start us, length us, event | category | flops | bytes accessed | tf_op | source)
XLA Modules:
  0.0 84.6 jit_solution(45704673168170906)
XLA Ops:
  0.6 1.5 %shard_map.104 = (f32[40,256]{1,0:T(8,128)S(1)}, f32[40,128]{1,0:T(8,128)S(1)}, f32[40,128]{1,0:T(8,128)S(1)}, f32[4,128]{1,0:T(4,128)S(1)}, f32[2,8,384]{2,1,0:...) custom-call(s32[1]{0:T(128)} %bitcast.1.gz_ref, f32[96,8]{1,0:T(8,128)} %bitcast.16, ...), custom_call_target="tpu_custom_call" | custom-call | flops 1000000 | bytes 100000 | tf_op jit(solution)/shard_map/pallas_call | solution.py:724
  2.1 8.3 %collective-permute-start = (f32[40,256]{1,0:T(8,128)S(1)}, f32[40,256]{1,0:T(8,128)S(1)}, u32[]{:S(2)}, u32[]{:S(2)}) collective-permute-start(f32[40,256]{1,0:T(8,128)S(1)} %get-tuple-element.26.own_ref), channel_id=1, source_target_pairs={{0,1},{1,0},{2,3},{3,2},{4,5},{5,4},{6,7},{7,6},{8,9},{9,8},{10,11... | collective-permute-start | bytes 122888 | tf_op jit(solution)/shard_map/ppermute | solution.py:757
  10.4 3.1 %collective-permute-start.1 = (f32[40,128]{1,0:T(8,128)S(1)}, f32[40,128]{1,0:T(8,128)S(1)}, u32[]{:S(2)}, u32[]{:S(2)}) collective-permute-start(f32[40,128]{1,0:T(8,128)S(1)} %get-tuple-element.27), channel_id=1, source_target_pairs={{0,2},{1,15},{2,4},{3,1},{4,6},{5,3},{6,8},{7,5},{8,10},{9,7},{10,... | collective-permute-start | bytes 61448 | tf_op jit(solution)/shard_map/ppermute | solution.py:755
  13.6 6.7 %collective-permute-start.2 = (f32[40,128]{1,0:T(8,128)S(1)}, f32[40,128]{1,0:T(8,128)S(1)}, u32[]{:S(2)}, u32[]{:S(2)}) collective-permute-start(f32[40,128]{1,0:T(8,128)S(1)} %get-tuple-element.28), channel_id=1, source_target_pairs={{0,15},{1,2},{2,1},{3,4},{4,3},{5,6},{6,5},{7,8},{8,7},{9,10},{10,... | collective-permute-start | bytes 61448 | tf_op jit(solution)/shard_map/ppermute | solution.py:756
  20.3 0.0 collective-permute-done.1.straight_ref
  20.3 2.3 %collective-permute-done.2.cross_ref = f32[40,128]{1,0:T(8,128)S(1)} collective-permute-done((f32[40,128]{1,0:T(8,128)S(1)}, f32[40,128]{1,0:T(8,128)S(1)}, u32[]{:S(2)}, u32[]{:S(2)}) %collective-permute-start.2) | collective-permute-done | bytes 20512 | tf_op jit(solution)/shard_map/ppermute | solution.py:756
  22.6 0.0 collective-permute-done.other_ref
  22.6 0.2 shard_map.105
  22.8 4.0 %collective-permute-start.3 = (f32[88,128]{1,0:T(8,128)S(1)}, f32[88,128]{1,0:T(8,128)S(1)}, u32[]{:S(2)}, u32[]{:S(2)}) collective-permute-start(f32[88,128]{1,0:T(8,128)S(1)} %get-tuple-element.30.rown_ref), channel_id=1, source_target_pairs={{0,16},{16,32},{32,48},{48,64},{64,80},{80,96},{96,112},{112,128},... | collective-permute-start | bytes 135176 | tf_op jit(solution)/shard_map/ppermute | solution.py:764
  26.8 10.8 %collective-permute-start.4 = (f32[88,128]{1,0:T(8,128)S(1)}, f32[88,128]{1,0:T(8,128)S(1)}, u32[]{:S(2)}, u32[]{:S(2)}) collective-permute-start(f32[88,128]{1,0:T(8,128)S(1)} %get-tuple-element.29.lown_ref), channel_id=1, source_target_pairs={{16,0},{32,16},{48,32},{64,48},{80,64},{96,80},{112,96},{128,112},... | collective-permute-start | bytes 135176 | tf_op jit(solution)/shard_map/ppermute | solution.py:765
  37.6 0.6 shard_map.106
  38.2 0.0 collective-permute-done.3.froml_ref
  38.2 0.5 collective-permute-done.4.fromr_ref
  38.7 21.7 %shard_map.107 = (f32[24,128]{1,0:T(8,128)S(1)}, f32[24,128]{1,0:T(8,128)S(1)}, f32[24,128]{1,0:T(8,128)S(1)}) custom-call(f32[88,128]{1,0:T(8,128)S(1)} %get-tuple-element.29.lown_ref, f32[88,128]{1,0:T(8,128)S(1)} %get-tuple-element.30.rown_ref, f32[88,128]{1,0:T(8,128)S(1)} %collective-permute-done.3.froml_ref, ...), custom_call_target="tpu_custom_call" | custom-call | flops 1000000000 | bytes 100000 | tf_op jit(solution)/shard_map/pallas_call | solution.py:816
  60.4 1.9 %collective-permute-start.5 = (f32[24,128]{1,0:T(8,128)S(1)}, f32[24,128]{1,0:T(8,128)S(1)}, u32[]{:S(2)}, u32[]{:S(2)}) collective-permute-start(f32[24,128]{1,0:T(8,128)S(1)} %get-tuple-element.46), channel_id=1, source_target_pairs={{0,16},{16,32},{32,48},{48,64},{64,80},{80,96},{96,112},{112,128},... | collective-permute-start | bytes 36872 | tf_op jit(solution)/shard_map/ppermute | solution.py:821
  62.4 7.0 %collective-permute-start.6 = (f32[24,128]{1,0:T(8,128)S(1)}, f32[24,128]{1,0:T(8,128)S(1)}, u32[]{:S(2)}, u32[]{:S(2)}) collective-permute-start(f32[24,128]{1,0:T(8,128)S(1)} %get-tuple-element.47), channel_id=1, source_target_pairs={{16,0},{32,16},{48,32},{64,48},{80,64},{96,80},{112,96},{128,112},... | collective-permute-start | bytes 36872 | tf_op jit(solution)/shard_map/ppermute | solution.py:820
  69.4 0.0 collective-permute-done.5.left_ref
  69.4 0.8 collective-permute-done.6.right_ref
  70.2 0.1 shard_map.108
  70.3 13.3 %all_to_all.5.got_ref = f32[16,8,128]{2,1,0:T(8,128)S(1)} all-to-all(f32[16,8,128]{2,1,0:T(8,128)S(1)} %shard_map.108), channel_id=1, replica_groups=mesh['gx'=32,'gy'=8,'gz'=2] {'gy','gz'}, dimensions={0} | all-to-all | bytes 131072 | tf_op jit(solution)/shard_map/all_to_all | solution.py:823
  83.6 1.0 %shard_map.109 = (f32[32,8]{1,0:T(8,128)}, f32[96,8]{1,0:T(8,128)}) custom-call(s32[1]{0:T(128)} %bitcast.gy_ref, f32[16,8,128]{2,1,0:T(8,128)S(1)} %all_to_all.5.got_ref), custom_call_target="tpu_custom_call" | custom-call | flops 1000000 | bytes 100000 | tf_op jit(solution)/shard_map/pallas_call | solution.py:824
Async XLA Ops:
  2.1 20.4 %collective-permute-start = (f32[40,256]{1,0:T(8,128)S(1)}, f32[40,256]{1,0:T(8,128)S(1)}, u32[]{:S(2)}, u32[]{:S(2)}) collective-permute-start(f32[40,256]{1,0:T(8,128)S(1)} %get-tuple-element.26.own_ref), channel_id=1, source_target_pairs={{0,1},{1,0},{2,3},{3,2},{4,5},{5,4},{6,7},{7,6},{8,9},{9,8},{10,11... | collective-permute-start | bytes 122888 | tf_op jit(solution)/shard_map/ppermute | solution.py:757
  10.4 9.9 %collective-permute-start.1 = (f32[40,128]{1,0:T(8,128)S(1)}, f32[40,128]{1,0:T(8,128)S(1)}, u32[]{:S(2)}, u32[]{:S(2)}) collective-permute-start(f32[40,128]{1,0:T(8,128)S(1)} %get-tuple-element.27), channel_id=1, source_target_pairs={{0,2},{1,15},{2,4},{3,1},{4,6},{5,3},{6,8},{7,5},{8,10},{9,7},{10,... | collective-permute-start | bytes 61448 | tf_op jit(solution)/shard_map/ppermute | solution.py:755
  13.6 9.0 %collective-permute-start.2 = (f32[40,128]{1,0:T(8,128)S(1)}, f32[40,128]{1,0:T(8,128)S(1)}, u32[]{:S(2)}, u32[]{:S(2)}) collective-permute-start(f32[40,128]{1,0:T(8,128)S(1)} %get-tuple-element.28), channel_id=1, source_target_pairs={{0,15},{1,2},{2,1},{3,4},{4,3},{5,6},{6,5},{7,8},{8,7},{9,10},{10,... | collective-permute-start | bytes 61448 | tf_op jit(solution)/shard_map/ppermute | solution.py:756
  22.8 15.4 %collective-permute-start.3 = (f32[88,128]{1,0:T(8,128)S(1)}, f32[88,128]{1,0:T(8,128)S(1)}, u32[]{:S(2)}, u32[]{:S(2)}) collective-permute-start(f32[88,128]{1,0:T(8,128)S(1)} %get-tuple-element.30.rown_ref), channel_id=1, source_target_pairs={{0,16},{16,32},{32,48},{48,64},{64,80},{80,96},{96,112},{112,128},... | collective-permute-start | bytes 135176 | tf_op jit(solution)/shard_map/ppermute | solution.py:764
  26.8 11.9 %collective-permute-start.4 = (f32[88,128]{1,0:T(8,128)S(1)}, f32[88,128]{1,0:T(8,128)S(1)}, u32[]{:S(2)}, u32[]{:S(2)}) collective-permute-start(f32[88,128]{1,0:T(8,128)S(1)} %get-tuple-element.29.lown_ref), channel_id=1, source_target_pairs={{16,0},{32,16},{48,32},{64,48},{80,64},{96,80},{112,96},{128,112},... | collective-permute-start | bytes 135176 | tf_op jit(solution)/shard_map/ppermute | solution.py:765
  60.4 8.9 %collective-permute-start.5 = (f32[24,128]{1,0:T(8,128)S(1)}, f32[24,128]{1,0:T(8,128)S(1)}, u32[]{:S(2)}, u32[]{:S(2)}) collective-permute-start(f32[24,128]{1,0:T(8,128)S(1)} %get-tuple-element.46), channel_id=1, source_target_pairs={{0,16},{16,32},{32,48},{48,64},{64,80},{80,96},{96,112},{112,128},... | collective-permute-start | bytes 36872 | tf_op jit(solution)/shard_map/ppermute | solution.py:821
  62.4 7.8 %collective-permute-start.6 = (f32[24,128]{1,0:T(8,128)S(1)}, f32[24,128]{1,0:T(8,128)S(1)}, u32[]{:S(2)}, u32[]{:S(2)}) collective-permute-start(f32[24,128]{1,0:T(8,128)S(1)} %get-tuple-element.47), channel_id=1, source_target_pairs={{16,0},{32,16},{48,32},{64,48},{80,64},{96,80},{112,96},{128,112},... | collective-permute-start | bytes 36872 | tf_op jit(solution)/shard_map/ppermute | solution.py:820
